TPU v7x, 32 devices: a whole 2x2x4 slice. The times are simulated.
32 devices in a mesh: expert: 8 (over z, x), shard: 4 (over y, core).
Axes of the slice: x: 2, y: 2, z: 4, core: 2. Of those that a mesh axis runs over, the one named last changes fastest.
Arguments:
- tokens_in: bfloat16 [4096, 2048], P(('expert', 'shard')), may hold values from -6 to 6
- out_grad: bfloat16 [4096, 2048], P(('expert', 'shard')), may hold values from -6 to 6
- segment_ids: int32 [8, 512], P('expert'), may hold values from 0 to 3, never falling along the last dimension, each value on 1 to 256 neighbouring positions
- expert_ids: int32 [4096, 8], P(('expert', 'shard')), may hold values from 0 to 31, all different within a row; in each aligned block of 128 rows (0 to 127, 128 to 255, ...) at most 64 rows name the same one
- route_weights: float32 [4096, 8], P(('expert', 'shard')), may hold values from 0.2 to 0.6
- attn_gain: bfloat16 [2048], P(('expert', 'shard')), may hold values from 0.5 to 2
- qkv_weight: bfloat16 [2048, 5120], P(('expert', 'shard')), may hold values from -0.125 to 0.125
- q_gain: bfloat16 [128], P(('expert', 'shard')), may hold values from 0.5 to 2
- k_gain: bfloat16 [128], P(('expert', 'shard')), may hold values from 0.5 to 2
- out_weight: bfloat16 [4096, 2048], P(('expert', 'shard')), may hold values from -0.75 to 0.75
- moe_gain: bfloat16 [2048], P(('expert', 'shard')), may hold values from 0.5 to 2
- expert_in: bfloat16 [32, 2048, 1536], P(('expert', 'shard')), may hold values from -0.125 to 0.125
- expert_out: bfloat16 [32, 768, 2048], P(('expert', 'shard')), may hold values from -0.4375 to 0.4375
Outputs:
- block_output: bfloat16 [4096, 2048], P(('expert', 'shard'))
- input_grad: bfloat16 [4096, 2048], P(('expert', 'shard'))
- attn_gain_grad: float32 [2048], P(('expert', 'shard'))
- qkv_weight_grad: float32 [2048, 5120], P(('expert', 'shard'))
- q_gain_grad: float32 [128], P(('expert', 'shard'))
- k_gain_grad: float32 [128], P(('expert', 'shard'))
- out_weight_grad: float32 [4096, 2048], P(('expert', 'shard'))
- moe_gain_grad: float32 [2048], P(('expert', 'shard'))
- expert_in_grad: float32 [32, 2048, 1536], P(('expert', 'shard'))
- expert_out_grad: float32 [32, 768, 2048], P(('expert', 'shard'))
Inputs may be any that keep to these rules, and one draw needn't show every extreme that they name: `segment_ids`: within each pack the document numbers never fall; each document covers 1 to 256 tokens and one covers exactly 256. `expert_ids`: each token names 8 different experts. Among the 128 tokens of one device no expert is named more than 64 times, a bound that some block reaches.
All inputs are finite; a program needn't handle non-finite values.
Results may differ from a plain program's by a relative error of at most 0.022.
Values may be sent and summed in bfloat16 or wider, within the bound.
A program may use at most 384 MiB of HBM per device.

v0:
```python
import math

import jax
import jax.numpy as jnp
from jax import lax
from jax.sharding import PartitionSpec as P

QUERY_HEADS = 32
KEY_VALUE_HEADS = 4
HEAD_DIMENSION = 128


EPSILON = 1e-06
THETA = 1000000.0


def norm_rows(values_in, gain):
    return (
        values_in
        * lax.rsqrt(jnp.mean(values_in * values_in, axis=-1, keepdims=True) + EPSILON)
        * gain
    )


def rotate(vectors, position):
    half_size = vectors.shape[-1] // 2
    freqs = jnp.exp(
        jnp.arange(half_size, dtype=jnp.float32) * (-2.0 * math.log(THETA) / vectors.shape[-1])
    )
    angles = position[:, None] * freqs[None, :]
    cosine = jnp.cos(angles)[:, None, :]
    sine = jnp.sin(angles)[:, None, :]
    first = vectors[..., :half_size]
    second = vectors[..., half_size:]
    return jnp.concatenate(
        [first * cosine - second * sine, second * cosine + first * sine], axis=-1
    )


def prepare(query_raw, unrotated_key, query_gain, key_gain, position):
    return (
        rotate(norm_rows(query_raw, query_gain), position),
        rotate(norm_rows(unrotated_key, key_gain), position),
    )


def segment_positions(segment):
    index = jnp.arange(segment.shape[0], dtype=jnp.int32)
    change = jnp.concatenate([jnp.ones((1,), dtype=bool), segment[1:] != segment[:-1]])
    start = lax.cummax(jnp.where(change, index, 0), axis=0)
    return index - start


def scores_of(queries, key_row_block, allowed):
    tok_count, heads, head_size = queries.shape
    kv_heads = key_row_block.shape[1]
    grouped = queries.reshape(tok_count, kv_heads, heads // kv_heads, head_size)
    scores = jnp.einsum(
        "tkgd,skd->kgts", grouped, key_row_block, preferred_element_type=jnp.float32
    ) * head_size ** (-0.5)
    return (jnp.where(allowed[None, None], scores, -1e30), grouped)


def attend(queries, key_row_block, value_row_block, allowed):
    scores, grouped = scores_of(queries, key_row_block, allowed)
    highest = jnp.max(scores, axis=-1, keepdims=True)
    log_total = highest + jnp.log(jnp.sum(jnp.exp(scores - highest), axis=-1, keepdims=True))
    probs = jnp.exp(scores - log_total).astype(jnp.bfloat16)
    mixed = jnp.einsum("kgts,skd->tkgd", probs, value_row_block, preferred_element_type=jnp.float32)
    return (mixed.reshape(queries.shape[0], -1).astype(jnp.bfloat16), log_total)


def attend_back(queries, key_row_block, value_row_block, allowed, log_total, attn_out, attn_grad):
    tok_count, heads, head_size = queries.shape
    kv_heads = key_row_block.shape[1]
    scores, grouped = scores_of(queries, key_row_block, allowed)
    probs = jnp.exp(scores - log_total)
    probs_low = probs.astype(jnp.bfloat16)
    grad_heads = attn_grad.reshape(tok_count, kv_heads, heads // kv_heads, head_size)
    out_heads = attn_out.reshape(tok_count, kv_heads, heads // kv_heads, head_size)
    delta = jnp.einsum("tkgd,tkgd->kgt", grad_heads, out_heads, preferred_element_type=jnp.float32)
    prob_grad = jnp.einsum(
        "tkgd,skd->kgts", grad_heads, value_row_block, preferred_element_type=jnp.float32
    )
    score_grad = (probs * (prob_grad - delta[..., None])).astype(jnp.bfloat16)
    factor = head_size ** (-0.5)
    query_grad = (
        jnp.einsum(
            "kgts,skd->tkgd", score_grad, key_row_block, preferred_element_type=jnp.float32
        ).reshape(tok_count, heads, head_size)
        * factor
    )
    key_gradient = (
        jnp.einsum("kgts,tkgd->skd", score_grad, grouped, preferred_element_type=jnp.float32)
        * factor
    )
    value_grad = jnp.einsum(
        "kgts,tkgd->skd", probs_low, grad_heads, preferred_element_type=jnp.float32
    )
    return (query_grad, key_gradient, value_grad)


def expert_step(rows_in, row_grads, weight_in, weight_out):
    hidden_size = weight_out.shape[0]
    pre = jnp.dot(rows_in, weight_in, preferred_element_type=jnp.float32)
    gate_part = pre[:, :hidden_size]
    up_part = pre[:, hidden_size:]
    sigma = jax.nn.sigmoid(gate_part)
    active = gate_part * sigma
    hidden = (active * up_part).astype(jnp.bfloat16)
    outputs = jnp.dot(hidden, weight_out, preferred_element_type=jnp.float32).astype(jnp.bfloat16)
    hidden_grad = jnp.einsum("rd,fd->rf", row_grads, weight_out, preferred_element_type=jnp.float32)
    gate_grad = hidden_grad * up_part * (sigma * (1.0 + gate_part * (1.0 - sigma)))
    up_grad = hidden_grad * active
    pre_grad = jnp.concatenate([gate_grad, up_grad], axis=-1).astype(jnp.bfloat16)
    rows_grad = jnp.einsum(
        "rc,dc->rd", pre_grad, weight_in, preferred_element_type=jnp.float32
    ).astype(jnp.bfloat16)
    return (outputs, rows_grad, pre_grad, hidden)


def shards(
    tokens_in,
    out_grad,
    segment_ids,
    expert_ids,
    route_weights,
    attn_gain,
    qkv_weight,
    q_gain,
    k_gain,
    out_weight,
    moe_gain,
    expert_in,
    expert_out,
):
    token_rows = tokens_in.shape[0]
    model_width = tokens_in.shape[1]
    gathered = (
        lax.all_gather(attn_gain, ("expert", "shard"), axis=0, tiled=True),
        lax.all_gather(qkv_weight, ("expert", "shard"), axis=0, tiled=True),
        lax.all_gather(q_gain, ("expert", "shard"), axis=0, tiled=True),
        lax.all_gather(k_gain, ("expert", "shard"), axis=0, tiled=True),
        lax.all_gather(out_weight, ("expert", "shard"), axis=0, tiled=True),
        lax.all_gather(moe_gain, ("expert", "shard"), axis=0, tiled=True),
    )
    attn_scale = gathered[0].astype(jnp.float32)
    qkv_full = gathered[1]
    query_gain = gathered[2].astype(jnp.float32)
    key_gain = gathered[3].astype(jnp.float32)
    out_full = gathered[4]
    moe_scale = gathered[5].astype(jnp.float32)
    block_f32 = tokens_in.astype(jnp.float32)
    normed_in = norm_rows(block_f32, attn_scale).astype(jnp.bfloat16)
    projected_rows = jnp.dot(normed_in, qkv_full, preferred_element_type=jnp.float32)
    query_raw = projected_rows[:, : QUERY_HEADS * HEAD_DIMENSION].reshape(
        token_rows, QUERY_HEADS, HEAD_DIMENSION
    )
    unrotated_key = projected_rows[
        :, QUERY_HEADS * HEAD_DIMENSION : (QUERY_HEADS + KEY_VALUE_HEADS) * HEAD_DIMENSION
    ].reshape(token_rows, KEY_VALUE_HEADS, HEAD_DIMENSION)
    value_reduced_precision = projected_rows[
        :, (QUERY_HEADS + KEY_VALUE_HEADS) * HEAD_DIMENSION :
    ].astype(jnp.bfloat16)
    segment_all = segment_ids[0]
    packed_length = segment_all.shape[0]
    offset = lax.axis_index("shard") * token_rows
    position = lax.dynamic_slice_in_dim(segment_positions(segment_all), offset, token_rows).astype(
        jnp.float32
    )
    segment_here = lax.dynamic_slice_in_dim(segment_all, offset, token_rows)

    def prepare_here(query_in, key_in, gain_q, gain_k):
        return prepare(query_in, key_in, gain_q, gain_k, position)

    query_rot, key_rot = prepare_here(query_raw, unrotated_key, query_gain, key_gain)
    query_low = query_rot.astype(jnp.bfloat16)
    key_value_width = KEY_VALUE_HEADS * HEAD_DIMENSION
    local_kv = jnp.concatenate(
        [
            key_rot.astype(jnp.bfloat16).reshape(token_rows, key_value_width),
            value_reduced_precision,
        ],
        axis=1,
    )
    gathered_key_value = lax.all_gather(local_kv, "shard", axis=0, tiled=True)
    key_row_block = gathered_key_value[:, :key_value_width].reshape(
        packed_length, KEY_VALUE_HEADS, HEAD_DIMENSION
    )
    value_row_block = gathered_key_value[:, key_value_width:].reshape(
        packed_length, KEY_VALUE_HEADS, HEAD_DIMENSION
    )
    query_index = offset + jnp.arange(token_rows, dtype=jnp.int32)
    key_index = jnp.arange(packed_length, dtype=jnp.int32)
    allowed = (segment_here[:, None] == segment_all[None, :]) & (
        key_index[None, :] <= query_index[:, None]
    )
    attn_out, log_total = attend(query_low, key_row_block, value_row_block, allowed)
    hidden_state = block_f32 + jnp.dot(attn_out, out_full, preferred_element_type=jnp.float32)
    moe_in = norm_rows(hidden_state, moe_scale).astype(jnp.bfloat16)
    grad_f32 = out_grad.astype(jnp.float32)
    route_count = expert_ids.shape[1]
    n_expert = lax.axis_size("expert")
    n_shard = lax.axis_size("shard")
    expert_total = n_expert * n_shard * expert_in.shape[0]
    slot_cap = max(2, 2 * token_rows * route_count // expert_total)
    flat_ids = expert_ids.reshape(-1)
    one_hot = (flat_ids[:, None] == jnp.arange(expert_total, dtype=jnp.int32)[None, :]).astype(
        jnp.int32
    )
    slot_rank = jnp.sum((jnp.cumsum(one_hot, axis=0) - 1) * one_hot, axis=1)
    slot_index = flat_ids * slot_cap + slot_rank
    route_grad = (route_weights[:, :, None] * grad_f32[:, None, :]).astype(jnp.bfloat16)
    route_grad = route_grad.reshape(token_rows * route_count, model_width)
    route_rows = jnp.repeat(moe_in, route_count, axis=0)
    send_rows = (
        jnp.zeros((expert_total * slot_cap, model_width), jnp.bfloat16)
        .at[slot_index]
        .set(route_rows)
    )
    send_grads = (
        jnp.zeros((expert_total * slot_cap, model_width), jnp.bfloat16)
        .at[slot_index]
        .set(route_grad)
    )
    send_rows = send_rows.reshape(expert_total, slot_cap, model_width)
    send_grads = send_grads.reshape(expert_total, slot_cap, model_width)
    got_rows, got_grads = (
        lax.all_to_all(send_rows, ("expert", "shard"), split_axis=0, concat_axis=1, tiled=True),
        lax.all_to_all(send_grads, ("expert", "shard"), split_axis=0, concat_axis=1, tiled=True),
    )
    got_rows = got_rows.reshape(-1, model_width)
    got_grads = got_grads.reshape(-1, model_width)
    outputs, rows_grad, pre_grad, hidden = expert_step(
        got_rows, got_grads, expert_in[0], expert_out[0]
    )
    expert_in_grad = jnp.einsum(
        "rd,rc->dc", got_rows, pre_grad, preferred_element_type=jnp.float32
    )[None]
    expert_out_grad = jnp.einsum(
        "rf,rd->fd", hidden, got_grads, preferred_element_type=jnp.float32
    )[None]
    back_out, back_grad = (
        lax.all_to_all(outputs[None], ("expert", "shard"), split_axis=1, concat_axis=0, tiled=True),
        lax.all_to_all(
            rows_grad[None], ("expert", "shard"), split_axis=1, concat_axis=0, tiled=True
        ),
    )
    back_out = back_out.reshape(expert_total * slot_cap, model_width)[slot_index]
    back_grad = back_grad.reshape(expert_total * slot_cap, model_width)[slot_index]
    back_out = back_out.reshape(token_rows, route_count, model_width).astype(jnp.float32)
    moe_sum = jnp.sum(route_weights[:, :, None] * back_out, axis=1)
    block_output = (hidden_state + moe_sum).astype(jnp.bfloat16)
    moe_grad = jnp.sum(
        back_grad.reshape(token_rows, route_count, model_width).astype(jnp.float32), axis=1
    )
    norm_out, norm_back = jax.vjp(norm_rows, hidden_state, moe_scale)
    hidden_grad, moe_scale_grad = norm_back(moe_grad)
    residual_grad = grad_f32 + hidden_grad
    residual_low = residual_grad.astype(jnp.bfloat16)
    out_weight_grad = lax.psum_scatter(
        jnp.einsum("tc,td->cd", attn_out, residual_low, preferred_element_type=jnp.float32),
        ("expert", "shard"),
        scatter_dimension=0,
        tiled=True,
    )
    attn_grad = jnp.einsum(
        "td,cd->tc", residual_low, out_full, preferred_element_type=jnp.float32
    ).astype(jnp.bfloat16)
    query_grad, key_grad_all, value_grad_all = attend_back(
        query_low, key_row_block, value_row_block, allowed, log_total, attn_out, attn_grad
    )
    kv_grad_all = jnp.concatenate(
        [
            key_grad_all.reshape(packed_length, key_value_width),
            value_grad_all.reshape(packed_length, key_value_width),
        ],
        axis=1,
    )
    key_value_gradient = lax.psum_scatter(
        kv_grad_all.astype(jnp.bfloat16), "shard", scatter_dimension=0, tiled=True
    ).astype(jnp.float32)
    key_gradient = key_value_gradient[:, :key_value_width].reshape(
        token_rows, KEY_VALUE_HEADS, HEAD_DIMENSION
    )
    value_grad = key_value_gradient[:, key_value_width:]
    prep_out, prep_back = jax.vjp(prepare_here, query_raw, unrotated_key, query_gain, key_gain)
    query_raw_grad, key_raw_grad, query_gain_grad, key_gain_grad = prep_back(
        (query_grad, key_gradient)
    )
    projected_grad = jnp.concatenate(
        [query_raw_grad.reshape(token_rows, -1), key_raw_grad.reshape(token_rows, -1), value_grad],
        axis=1,
    ).astype(jnp.bfloat16)
    qkv_term = jnp.einsum(
        "td,tc->dc", normed_in, projected_grad, preferred_element_type=jnp.float32
    )
    normed_grad = jnp.einsum(
        "tc,dc->td", projected_grad, qkv_full, preferred_element_type=jnp.float32
    )
    first_out, first_back = jax.vjp(norm_rows, block_f32, attn_scale)
    input_part, attn_scale_grad = first_back(normed_grad)
    input_grad = (residual_grad + input_part).astype(jnp.bfloat16)
    summed = (
        lax.psum_scatter(attn_scale_grad, ("expert", "shard"), scatter_dimension=0, tiled=True),
        lax.psum_scatter(qkv_term, ("expert", "shard"), scatter_dimension=0, tiled=True),
        lax.psum_scatter(query_gain_grad, ("expert", "shard"), scatter_dimension=0, tiled=True),
        lax.psum_scatter(key_gain_grad, ("expert", "shard"), scatter_dimension=0, tiled=True),
        lax.psum_scatter(moe_scale_grad, ("expert", "shard"), scatter_dimension=0, tiled=True),
    )
    return (
        block_output,
        input_grad,
        summed[0],
        summed[1],
        summed[2],
        summed[3],
        out_weight_grad,
        summed[4],
        expert_in_grad,
        expert_out_grad,
    )


def solution(mesh):
    placed = (
        P(("expert", "shard"), None),
        P(("expert", "shard"), None),
        P("expert", None),
        P(("expert", "shard"), None),
        P(("expert", "shard"), None),
        P(("expert", "shard")),
        P(("expert", "shard"), None),
        P(("expert", "shard")),
        P(("expert", "shard")),
        P(("expert", "shard"), None),
        P(("expert", "shard")),
        P(("expert", "shard"), None, None),
        P(("expert", "shard"), None, None),
    )
    return jax.shard_map(
        shards,
        mesh=mesh,
        in_specs=placed,
        out_specs=(
            P(("expert", "shard"), None),
            P(("expert", "shard"), None),
            P(("expert", "shard")),
            P(("expert", "shard"), None),
            P(("expert", "shard")),
            P(("expert", "shard")),
            P(("expert", "shard"), None),
            P(("expert", "shard")),
            P(("expert", "shard"), None, None),
            P(("expert", "shard"), None, None),
        ),
        check_vma=False,
    )
```

profile of v0, /device:TPU:2, one launch (start us, length us, event | category | flops | bytes accessed | tf_op | source)
XLA Modules:
  0.0 2159.5 jit_solution(14982436753775393803)
XLA Ops:
  12.8 43.6 %all-reduce.13 = (bf16[2048]{0:T(1024)(128)(2,1)S(1)}, bf16[128]{0:T(256)(128)(2,1)S(1)}, bf16[128]{0:T(256)(128)(2,1)}, bf16[2048]{0:T(1024)(128)(2,1)}) all-reduce(bf16[2048]{0:T(1024)(128)(2,1)S(1)} %dynamic-update-slice, bf16[128]{0:T(256)(128)(2,1)S(1)} %dynamic-update-slice.1, ...), channel_id=1, replica_groups=mesh['expert'=8,'shard'=4] {'expert','shard'}, use_global_device_ids=true, to_apply=%add.4 | all-reduce | flops 4352 | bytes 17408
  59.3 87.9 %all-gather.4.cloned.1.call-done = bf16[2048,5120]{1,0:T(8,128)(2,1)} async-done(((bf16[64,5120]{1,0:T(8,128)(2,1)}), bf16[2048,5120]{1,0:T(8,128)(2,1)}) %all-gather.4.cloned.1.call-update) | async-done | bytes 20971536 | tf_op jit(solution)/shard_map/all_gather | solution.py:141
  147.2 8.7 fusion.48
  172.6 17.5 reduce-window.19
  213.2 3.8 fusion.9
  226.1 71.1 %all-gather.8.cloned.1.call-done = bf16[4096,2048]{1,0:T(8,128)(2,1)} async-done(((bf16[128,2048]{1,0:T(8,128)(2,1)}), bf16[4096,2048]{1,0:T(8,128)(2,1)}) %all-gather.8.cloned.1.call-update) | async-done | bytes 16777232 | tf_op jit(solution)/shard_map/all_gather | solution.py:144
  297.1 8.5 multiply_reduce_fusion.6
  307.6 12.4 scatter_custom_fusion
  320.0 4.5 all-to-all-start
  326.9 12.1 scatter_custom_fusion.1
  338.9 170.5 %all-to-all-done = bf16[32,64,2048]{2,1,0:T(8,128)(2,1)} async-done(((bf16[32,64,2048]{2,1,0:T(8,128)(2,1)}), bf16[32,64,2048]{2,1,0:T(8,128)(2,1)}, u32[]{:S(2)}, u32[]{:S(2)}) %all-to-all-start) | async-done | bytes 8388640 | tf_op jit(solution)/shard_map/all_to_all | solution.py:229
  509.4 8.2 all-to-all-start.2
  517.5 19.0 fusion.6
  536.6 165.7 %all-to-all-done.2 = bf16[32,64,2048]{2,1,0:T(8,128)(2,1)} async-done(((bf16[32,64,2048]{2,1,0:T(8,128)(2,1)}), bf16[32,64,2048]{2,1,0:T(8,128)(2,1)}, u32[]{:S(2)}, u32[]{:S(2)}) %all-to-all-start.2) | async-done | bytes 8388640 | tf_op jit(solution)/shard_map/all_to_all | solution.py:230
  702.3 15.7 multiply_convert_fusion.1
  718.0 19.6 convert_bitcast_fusion
  737.6 15.5 copy.239
  753.6 51.2 %reduce.6 = bf16[2048,2048]{1,0:T(8,128)(2,1)} reduce(bf16[2048,1,2048]{2,1,0:T(2,128)(2,1)} %bitcast.179, bf16[]{:T(256)} %broadcast.367), dimensions={1}, to_apply=%bitcast.169.reduce_sub_computation | reduce | bytes 16777218
  804.8 21.6 %reshape.465 = bf16[32,2,65536]{2,1,0:T(2,128)(2,1)} reshape(bf16[2048,2048]{1,0:T(8,128)(2,1)} %reduce.6) | data formatting | bytes 16777216
  826.4 8.6 all-to-all-start.3
  835.1 8.9 convert_bitcast_fusion.1
  844.0 48.4 %copy.240 = bf16[1,2048,2048]{2,0,1:T(2,128)(2,1)} copy(bf16[1,2048,2048]{2,1,0:T(8,128)(2,1)S(1)} %convert_bitcast_fusion.1) | data formatting | bytes 16777216 | tf_op jit(solution)/shard_map/broadcast_in_dim | solution.py:244
  892.3 51.2 %reduce.7 = bf16[2048,2048]{1,0:T(8,128)(2,1)} reduce(bf16[2048,1,2048]{2,1,0:T(2,128)(2,1)} %bitcast.180, bf16[]{:T(256)} %broadcast.367), dimensions={1}, to_apply=%bitcast.170.reduce_sub_computation | reduce | bytes 16777218
  943.5 21.6 reshape.463
  965.1 54.7 %all-to-all-done.3 = bf16[32,2,65536]{2,1,0:T(2,128)(2,1)} async-done(((bf16[32,2,65536]{2,1,0:T(2,128)(2,1)}), bf16[32,2,65536]{2,1,0:T(2,128)(2,1)}, u32[]{:S(2)}, u32[]{:S(2)}) %all-to-all-start.3) | async-done | bytes 8388640 | tf_op jit(solution)/shard_map/all_to_all | solution.py:245
  1019.8 8.0 all-to-all-start.1
  1027.8 8.1 copy.175
  1036.0 23.4 %reshape.466 = bf16[2048,1,2048]{2,1,0:T(2,128)(2,1)} reshape(bf16[32,2,65536]{2,1,0:T(2,128)(2,1)} %all-to-all-done.3) | data formatting | bytes 16777216
  1059.4 13.5 copy.234
  1072.8 139.9 %all-to-all-done.1 = bf16[32,2,65536]{2,1,0:T(2,128)(2,1)} async-done(((bf16[32,2,65536]{2,1,0:T(2,128)(2,1)}), bf16[32,2,65536]{2,1,0:T(2,128)(2,1)}, u32[]{:S(2)}, u32[]{:S(2)}) %all-to-all-start.1) | async-done | bytes 8388640 | tf_op jit(solution)/shard_map/all_to_all | solution.py:244
  1212.7 23.4 %reshape.464 = bf16[2048,1,2048]{2,1,0:T(2,128)(2,1)} reshape(bf16[32,2,65536]{2,1,0:T(2,128)(2,1)} %all-to-all-done.1) | data formatting | bytes 16777216
  1236.1 13.4 copy.235
  1249.5 13.3 gather_fusion.1
  1262.8 13.3 gather_fusion
  1276.1 8.8 convert_reduce_fusion
  1286.5 11.8 fusion.23
  1303.3 3.4 copy.190
  1308.6 6.8 fusion.2
  1320.6 13.6 fusion.42
  1339.4 4.2 copy.208
  1351.9 3.9 fusion.21
  1359.7 16.6 fusion.37
  1378.3 10.9 convolution_bitcast_fusion.1
  1389.2 17.5 convolution_bitcast_fusion
  1406.8 12.6 fusion.30
  1419.4 50.3 %all-reduce.12 = (f32[2048]{0:T(1024)S(1)}, f32[128]{0:T(128)S(1)}, f32[128]{0:T(128)S(1)}, f32[2048]{0:T(1024)S(1)}) all-reduce(f32[2048]{0:T(1024)S(1)} %get-tuple-element.14, f32[128]{0:T(128)S(1)} %get-tuple-element.10, f32[128]{0:T(128)S(1)} %get-tuple-element.16, ...), channel_id=3, replica_groups=mesh['expert'=8,'shard'=4] {'expert','shard'}, use_global_device_ids=true, to_apply=%region_21.22.clone | all-reduce | flops 4352 | bytes 34816
  1474.9 230.8 %reduce-scatter.8.cloned.1.call-done = f32[128,2048]{1,0:T(8,128)} async-done(((f32[4096,2048]{1,0:T(8,128)}), f32[128,2048]{1,0:T(8,128)}) %reduce-scatter.8.cloned.1.call-update) | async-done | bytes 1048592 | tf_op jit(solution)/shard_map/reduce_scatter | solution.py:261
  1705.7 446.7 %reduce-scatter.6.cloned.1.call-done = f32[64,5120]{1,0:T(8,128)} async-done(((f32[2048,5120]{1,0:T(8,128)}), f32[64,5120]{1,0:T(8,128)}) %reduce-scatter.6.cloned.1.call-update) | async-done | bytes 1310736 | tf_op jit(solution)/shard_map/reduce_scatter | solution.py:306
  (266 shorter events, 99.6 us)
Async XLA Ops:
  7.2 695.1 %copy-start = (bf16[1,768,2048]{2,1,0:T(8,128)(2,1)S(1)}, bf16[1,768,2048]{2,1,0:T(8,128)(2,1)}, u32[]{:S(2)}) copy-start(bf16[1,768,2048]{2,1,0:T(8,128)(2,1)} %param.25) | copy-start | bytes 9437188
  7.2 140.0 %all-gather.4.cloned.1.call-start = ((), (), s32[]{:S(2)}) async-start(), calls=%async_computation.7 | async-start | bytes 21626880 | tf_op jit(solution)/shard_map/all_gather | solution.py:141
  7.9 197.0 %all-gather.6.cloned.1.call-start = ((), (), s32[]{:S(2)}) async-start(), calls=%async_computation.8 | async-start | bytes 1310720 | tf_op jit(solution)/shard_map/all_gather | solution.py:186
  56.9 99.0 %copy-start.40 = (f32[2048]{0:T(1024)}, f32[2048]{0:T(1024)S(1)}, u32[]{:S(2)}) copy-start(f32[2048]{0:T(1024)S(1)} %convert_element_type.100) | copy-start | bytes 24580
  58.9 97.0 %copy-start.48 = (f32[128]{0:T(128)}, f32[128]{0:T(128)S(1)}, u32[]{:S(2)}) copy-start(f32[128]{0:T(128)S(1)} %fusion.55) | copy-start | bytes 1540
  59.3 103.5 %copy-start.32 = (f32[128,64]{1,0:T(8,128)}, f32[128,64]{1,0:T(8,128)S(1)}, u32[]{:S(2)}) copy-start(f32[128,64]{1,0:T(8,128)S(1)} %get-tuple-element.48) | copy-start | bytes 98308
  59.3 142.1 %copy-start.30 = (f32[128,64]{1,0:T(8,128)}, f32[128,64]{1,0:T(8,128)S(1)}, u32[]{:S(2)}) copy-start(f32[128,64]{1,0:T(8,128)S(1)} %get-tuple-element.47) | copy-start | bytes 98308
  155.9 9.8 copy-start.53
  155.9 36.9 %copy-start.52 = (s32[1,512]{1,0:T(1,128)S(1)}, s32[1,512]{1,0:T(1,128)}, u32[]{:S(2)}) copy-start(s32[1,512]{1,0:T(1,128)} %param.15) | copy-start | bytes 6148
  159.2 37.4 %copy-start.20 = (f32[128,4,128]{2,1,0:T(4,128)}, f32[128,4,128]{2,1,0:T(4,128)S(1)}, u32[]{:S(2)}) copy-start(f32[128,4,128]{2,1,0:T(4,128)S(1)} %reshape.382) | copy-start | bytes 786436
  161.0 6.8 copy-start.50
  165.0 132.2 %all-gather.8.cloned.1.call-start = ((), (), s32[]{:S(2)}) async-start(), calls=%async_computation.9 | async-start | bytes 17301504 | tf_op jit(solution)/shard_map/all_gather | solution.py:144
  168.5 137.3 %copy-start.44 = (f32[2048]{0:T(1024)}, f32[2048]{0:T(1024)S(1)}, u32[]{:S(2)}) copy-start(f32[2048]{0:T(1024)S(1)} %convert_element_type.111) | copy-start | bytes 24580
  194.8 24.1 %copy-start.28 = (pred[128,512]{0,1:T(8,128)(4,1)}, pred[128,512]{0,1:T(8,128)(4,1)S(1)}, u32[]{:S(2)}) copy-start(pred[128,512]{0,1:T(8,128)(4,1)S(1)} %fusion.45) | copy-start | bytes 196612
  197.0 4.4 copy-start.33
  305.7 14.3 copy-start.55
  320.0 4.5 copy-start.59
  320.0 189.3 %all-to-all-start = ((bf16[32,64,2048]{2,1,0:T(8,128)(2,1)}), bf16[32,64,2048]{2,1,0:T(8,128)(2,1)}, u32[]{:S(2)}, u32[]{:S(2)}) async-start(bf16[32,64,2048]{2,1,0:T(8,128)(2,1)} %bitcast.182), calls=%async_computation | async-start | bytes 16777216 | tf_op jit(solution)/shard_map/all_to_all | solution.py:229
  324.6 14.3 copy-start.38
  509.4 192.9 %all-to-all-start.2 = ((bf16[32,64,2048]{2,1,0:T(8,128)(2,1)}), bf16[32,64,2048]{2,1,0:T(8,128)(2,1)}, u32[]{:S(2)}, u32[]{:S(2)}) async-start(bf16[32,64,2048]{2,1,0:T(8,128)(2,1)} %bitcast.181), calls=%async_computation.2 | async-start | bytes 16777216 | tf_op jit(solution)/shard_map/all_to_all | solution.py:230
  718.0 19.6 copy-start.65
  826.4 193.4 %all-to-all-start.3 = ((bf16[32,2,65536]{2,1,0:T(2,128)(2,1)}), bf16[32,2,65536]{2,1,0:T(2,128)(2,1)}, u32[]{:S(2)}, u32[]{:S(2)}) async-start(bf16[32,2,65536]{2,1,0:T(2,128)(2,1)} %reshape.465), calls=%async_computation.3 | async-start | bytes 16777216 | tf_op jit(solution)/shard_map/all_to_all | solution.py:245
  1019.8 192.9 %all-to-all-start.1 = ((bf16[32,2,65536]{2,1,0:T(2,128)(2,1)}), bf16[32,2,65536]{2,1,0:T(2,128)(2,1)}, u32[]{:S(2)}, u32[]{:S(2)}) async-start(bf16[32,2,65536]{2,1,0:T(2,128)(2,1)} %reshape.463), calls=%async_computation.1 | async-start | bytes 16777216 | tf_op jit(solution)/shard_map/all_to_all | solution.py:244
  1027.8 328.7 %reduce-scatter.10.cloned.1.call-start = ((), (), s32[]{:S(2)}) async-start(), calls=%async_computation.12 | async-start | bytes 1310720
  1262.8 13.3 copy-start.39
  1276.1 8.9 copy-start.12
  1276.1 8.9 copy-start.45
  1276.1 8.9 copy-start.56
  1276.1 9.2 copy-start.63
  1276.1 9.2 copy-start.25
  1286.5 34.0 %copy-start.9 = (f32[128,2048]{1,0:T(8,128)}, f32[128,2048]{1,0:T(8,128)S(1)}, u32[]{:S(2)}) copy-start(f32[128,2048]{1,0:T(8,128)S(1)} %get-tuple-element.35) | copy-start | bytes 3145732
  1298.6 4.7 copy-start.19
  1301.7 5.0 copy-start.6
  1303.3 5.3 copy-start.29
  1303.3 5.3 copy-start.47
  1308.6 8.9 copy-start.17
  1308.6 8.9 copy-start.18
  1320.5 385.2 %reduce-scatter.8.cloned.1.call-start = ((), (), s32[]{:S(2)}) async-start(), calls=%async_computation.11 | async-start | bytes 34603008 | tf_op jit(solution)/shard_map/reduce_scatter | solution.py:261
  1334.2 818.2 %reduce-scatter.6.cloned.1.call-start = ((), (), s32[]{:S(2)}) async-start(), calls=%async_computation.10 | async-start | bytes 43253760 | tf_op jit(solution)/shard_map/reduce_scatter | solution.py:306
  1339.3 7.0 copy-start.31
  1339.4 7.0 copy-start.34
  1356.4 19.9 copy-start.23
  1378.3 10.9 copy-start.66
  1378.3 10.9 copy-start.67
  1389.2 17.6 copy-start.15
  1389.2 17.6 copy-start.24
  1406.8 65.2 %copy-start.61 = (f32[128]{0:T(128)S(1)}, f32[128]{0:T(128)}, u32[]{:S(2)}) copy-start(f32[128]{0:T(128)} %copy-done.60) | copy-start | bytes 1540
  1406.8 745.6 %copy-start.1 = (bf16[1,768,2048]{2,1,0:T(8,128)(2,1)S(1)}, bf16[1,768,2048]{2,1,0:T(8,128)(2,1)}, u32[]{:S(2)}) copy-start(bf16[1,768,2048]{2,1,0:T(8,128)(2,1)} %param.25) | copy-start | bytes 9437188
  (30 other events, 74.6 us)
Sparse Core Ops, SparseCore 0:
  10.8 136.2 all-gather.3
  165.1 14.9 all-gather.5
  182.9 114.1 all-gather.7
  1320.6 27.7 reduce-scatter.9
  1351.1 354.5 reduce-scatter.7
  1708.5 443.8 reduce-scatter.5
where the time goes:
time: 2180 us; the launch traced here: 2160 us
  waiting for transfers between devices  1370 us (63%)
  local copies, waits for them, and re-layouts  286 us (13%)
  other arithmetic  184 us (8%)
  matrix products  182 us (8%)
  blocking collectives  93.8 us (4%)
  starting transfers between devices  29.5 us (1%)
    reduce_scatter x1, waiting for transfers between devices, shards(): lax.psum_scatter(qkv_term, ('expert', 'shard'), scatter_dimension=0, tile...  447 us
    reduce_scatter x1, waiting for transfers between devices, shards(): lax.psum_scatter(jnp.einsum('tc,td->cd', attn_out, residual_low, preferre...  231 us
    all_to_all x1, waiting for transfers between devices, shards(): lax.all_to_all(send_rows, ('expert', 'shard'), split_axis=0, concat_axis=...  170 us
    all_to_all x1, waiting for transfers between devices, shards(): lax.all_to_all(send_grads, ('expert', 'shard'), split_axis=0, concat_axis...  166 us
    unnamed x170, local copies, waits for them, and re-layouts  152 us
    all_to_all x1, waiting for transfers between devices, shards(): lax.all_to_all(outputs[None], ('expert', 'shard'), split_axis=1, concat_a...  140 us
    unnamed x3, other arithmetic  104 us
    unnamed x2, blocking collectives  93.8 us
  transfers between devices with their start and end apart: 10, of which 8 were waited for; matrix products, arithmetic and copies ran while one was open for 17% of the time, Pallas kernels for 0%

commit v1 on v0

v1 whole, which is shorter than its diff:
```python
import math
import jax, jax.numpy as jnp
from jax import lax
from jax.experimental import pallas as pl
from jax.experimental.pallas import tpu as pltpu
from jax.sharding import PartitionSpec as P
MESH = pl.DeviceIdType.MESH
ANY = pl.BlockSpec(memory_space=pl.ANY)
VM = pl.BlockSpec(memory_space=pltpu.VMEM)

def grid_of():
    n_expert, n_shard = lax.axis_size("expert"), lax.axis_size("shard")
    ny = n_shard // 2
    nx = min(ny, n_expert)
    return n_expert // nx, nx, ny

class Place:
    def __init__(self):
        self.nz, self.nx, self.ny = grid_of()
        e, s = lax.axis_index("expert"), lax.axis_index("shard")
        self.z, self.x = e // self.nx, e % self.nx
        self.y, self.c = s // 2, s % 2
    def dev(self, dz=0, dx=0, dy=0, dc=0):
        z, x, y, c = self.at(dz, dx, dy, dc)
        return (z * self.nx + x, y * 2 + c)
    def at(self, dz=0, dx=0, dy=0, dc=0):
        z = lax.rem(self.z + dz + self.nz, self.nz) if dz else self.z
        x = lax.rem(self.x + dx + self.nx, self.nx) if dx else self.x
        y = lax.rem(self.y + dy + self.ny, self.ny) if dy else self.y
        c = 1 - self.c if dc else self.c
        return z, x, y, c
    def index(self, dz=0, dx=0, dy=0, dc=0):
        z, x, y, c = self.at(dz, dx, dy, dc)
        return ((z * self.nx + x) * self.ny + y) * 2 + c
    def greet(self, peers):
        barrier = pltpu.get_barrier_semaphore()
        for p in peers:
            pl.semaphore_signal(barrier, inc=1, device_id=self.dev(*p), device_id_type=MESH)
        pl.semaphore_wait(barrier, len(peers))
    def line_peers(self):
        return ([(d, 0, 0, 0) for d in range(1, self.nz)] + [(0, d, 0, 0) for d in range(1, self.nx)]
                + [(0, 0, d, 0) for d in range(1, self.ny)] + [(0, 0, 0, 1)])

class Pool:
    def __init__(self, sems):
        self.sems, self.used = sems, 0
    def take(self):
        self.used += 1
        return self.sems.at[self.used - 1]

def gather_all_kernel(b_ref, o_ref, local_sem, send, recv):
    p = Place()
    nz, nx, ny = p.nz, p.nx, p.ny
    half = b_ref.shape[0] // 2
    A, B = pl.ds(0, half), pl.ds(half, half)
    F = pl.ds(0, 2 * half)
    p.greet(p.line_peers())
    own = pltpu.make_async_copy(b_ref, o_ref.at[p.index()], local_sem)
    own.start()
    s, r = Pool(send), Pool(recv)
    sent = []
    def push(src_at, rows, to, first=False):
        i = p.index(*src_at)
        src = b_ref.at[rows] if first else o_ref.at[i, rows]
        cp = pltpu.make_async_remote_copy(src_ref=src, dst_ref=o_ref.at[i, rows], send_sem=s.take(),
            recv_sem=r.take(), device_id=p.dev(*to), device_id_type=MESH)
        cp.start()
        sent.append(cp)
        return cp
    neg = lambda d, n: (n - d) % n
    first = {}
    for d in range(1, nz):
        first[d] = push((0, 0, 0, 0), F, (d, 0, 0, 0), True)
    second_a, second_b, third, fourth = {}, {}, {}, []
    def stage_one(k):
        if k:
            first[k].wait_recv()
        at = (neg(k, nz), 0, 0, 0)
        for d in range(1, nx):
            second_a[k, d] = push(at, A, (0, d, 0, 0), k == 0)
        for d in range(1, ny):
            second_b[k, d] = push(at, B, (0, 0, d, 0), k == 0)
        for d in range(1, ny):
            third["a", k, 0, d] = push(at, A, (0, 0, d, 0), k == 0)
        for d in range(1, nx):
            third["b", k, 0, d] = push(at, B, (0, d, 0, 0), k == 0)
        fourth.append(push(at, F, (0, 0, 0, 1), k == 0))
    def stage_two(k):
        for dx in range(1, nx):
            second_a[k, dx].wait_recv()
            at = (neg(k, nz), neg(dx, nx), 0, 0)
            for d in range(1, ny):
                third["a", k, dx, d] = push(at, A, (0, 0, d, 0))
            fourth.append(push(at, A, (0, 0, 0, 1)))
        for dy in range(1, ny):
            second_b[k, dy].wait_recv()
            at = (neg(k, nz), 0, neg(dy, ny), 0)
            for d in range(1, nx):
                third["b", k, dy, d] = push(at, B, (0, d, 0, 0))
            fourth.append(push(at, B, (0, 0, 0, 1)))
    def stage_three(k):
        for dx in range(nx):
            for d in range(1, ny):
                third["a", k, dx, d].wait_recv()
                fourth.append(push((neg(k, nz), neg(dx, nx), neg(d, ny), 0), A, (0, 0, 0, 1)))
        for dy in range(ny):
            for d in range(1, nx):
                third["b", k, dy, d].wait_recv()
                fourth.append(push((neg(k, nz), neg(d, nx), neg(dy, ny), 0), B, (0, 0, 0, 1)))
    for k in range(nz + 2):
        if k < nz:
            stage_one(k)
        if 0 <= k - 1 < nz:
            stage_two(k - 1)
        if 0 <= k - 2 < nz:
            stage_three(k - 2)
    for cp in fourth:
        cp.wait_recv()
    for cp in sent:
        cp.wait_send()
    own.wait()

def gather_all(block, cid):
    nz, nx, ny = grid_of()
    return pl.pallas_call(gather_all_kernel,
        out_shape=jax.ShapeDtypeStruct((nz * nx * ny * 2,) + block.shape, block.dtype),
        in_specs=[VM], out_specs=ANY,
        scratch_shapes=[pltpu.SemaphoreType.DMA, pltpu.SemaphoreType.DMA((n_sems(nz, nx, ny),)), pltpu.SemaphoreType.DMA((n_sems(nz, nx, ny),))],
        compiler_params=pltpu.CompilerParams(collective_id=cid, has_side_effects=True),
        name="gather_all")(block)

def n_sems(nz, nx, ny):
    return (nz - 1) + nz * (nx - 1 + ny - 1 + 1) + nz * (nx * (ny - 1) + ny * (nx - 1)) + nz * (nx - 1 + ny - 1) + nz * (nx * (ny - 1) + ny * (nx - 1))

def reduce_all_kernel(g_ref, out_ref, acc, rc, ra1, rb1, ra2, rb2, rz, load_sem, send, recv):
    p = Place()
    nz, nx, ny = p.nz, p.nx, p.ny
    rows = g_ref.shape[1]
    half = rows // 2
    A, B = pl.ds(0, half), pl.ds(half, half)
    p.greet(p.line_peers())
    s, r = Pool(send), Pool(recv)
    sent = []
    order = [(dz, dx, dy) for dx in reversed(range(nx)) for dy in reversed(range(ny)) for dz in range(nz)]
    slot = lambda dz, dx, dy: (dz * nx + dx) * ny + dy
    neg = lambda d, n: (n - d) % n
    def push(src, dst, to):
        cp = pltpu.make_async_remote_copy(src_ref=src, dst_ref=dst, send_sem=s.take(), recv_sem=r.take(),
            device_id=p.dev(*to), device_id_type=MESH)
        cp.start()
        sent.append(cp)
        return cp
    loads, cores = {}, {}
    zs = list(range(1, nz)) + [0]
    plane = [(dx, dy) for dx in reversed(range(nx)) for dy in reversed(range(ny))]
    for dz in zs:
        for dx, dy in plane:
            k = (dz, dx, dy)
            i = slot(*k)
            cores[k] = push(g_ref.at[p.index(*k, 1)], rc.at[i], (0, 0, 0, 1))
            loads[k] = pltpu.make_async_copy(g_ref.at[p.index(*k)], acc.at[i], load_sem.at[i])
            loads[k].start()
    def add(dst, rows_, src):
        dst_v = acc[dst, rows_, :].astype(jnp.float32) + src[...].astype(jnp.float32)
        acc[dst, rows_, :] = dst_v.astype(acc.dtype)
    ca, cb, za, zb, zz = {}, {}, {}, {}, {}
    def stage_one(dz):
        for dx, dy in plane:
            k = (dz, dx, dy)
            i = slot(*k)
            loads[k].wait()
            cores[k].wait_recv()
            acc[i] = (acc[i].astype(jnp.float32) + rc[i].astype(jnp.float32)).astype(acc.dtype)
            if dy:
                ca[k] = push(acc.at[i, A], ra1.at[dy - 1, dz * nx + dx], (0, 0, dy, 0))
            if dx:
                cb[k] = push(acc.at[i, B], rb1.at[dx - 1, dz * ny + dy], (0, dx, 0, 0))
    def stage_two(dz):
        for dx in reversed(range(nx)):
            for dy in range(1, ny):
                ca[dz, dx, dy].wait_recv()
                add(slot(dz, dx, 0), A, ra1.at[dy - 1, dz * nx + dx])
            if dx:
                za[dz, dx] = push(acc.at[slot(dz, dx, 0), A], ra2.at[dx - 1, dz], (0, dx, 0, 0))
        for dy in reversed(range(ny)):
            for dx in range(1, nx):
                cb[dz, dx, dy].wait_recv()
                add(slot(dz, 0, dy), B, rb1.at[dx - 1, dz * ny + dy])
            if dy:
                zb[dz, dy] = push(acc.at[slot(dz, 0, dy), B], rb2.at[dy - 1, dz], (0, 0, dy, 0))
    def stage_three(dz):
        for dx in range(1, nx):
            za[dz, dx].wait_recv()
            add(slot(dz, 0, 0), A, ra2.at[dx - 1, dz])
        for dy in range(1, ny):
            zb[dz, dy].wait_recv()
            add(slot(dz, 0, 0), B, rb2.at[dy - 1, dz])
        if dz:
            zz[dz] = push(acc.at[slot(dz, 0, 0)], rz.at[dz - 1], (dz, 0, 0, 0))
    for k in range(nz + 2):
        if k < nz:
            stage_one(zs[k])
        if 0 <= k - 1 < nz:
            stage_two(zs[k - 1])
        if 0 <= k - 2 < nz:
            stage_three(zs[k - 2])
    total = acc[slot(0, 0, 0)].astype(jnp.float32)
    for dz in range(1, nz):
        zz[dz].wait_recv()
        total = total + rz[dz - 1].astype(jnp.float32)
    out_ref[...] = total.astype(out_ref.dtype)
    for cp in sent:
        cp.wait_send()

def reduce_all(terms, dtype, cid):
    nz, nx, ny = grid_of()
    nd, rows, width = terms.shape
    dt = terms.dtype
    half = rows // 2
    n = nz * nx * ny + 2 * nz * nx * ny + nz * (nx + ny) + nz
    blocks = 2 * nz * nx * ny + nz + (nz * (nx + 1) * (ny - 1) + nz * (ny + 1) * (nx - 1)) // 2 + 4
    parts = 1
    while blocks * rows * width * 2 // parts > 54 << 20:
        parts *= 2
    cols = width // parts
    one = pl.pallas_call(reduce_all_kernel,
        out_shape=jax.ShapeDtypeStruct((rows, cols), dtype),
        in_specs=[ANY], out_specs=VM,
        scratch_shapes=[pltpu.VMEM((nz * nx * ny, rows, cols), dt), pltpu.VMEM((nz * nx * ny, rows, cols), dt),
            pltpu.VMEM((ny - 1, nz * nx, half, cols), dt), pltpu.VMEM((nx - 1, nz * ny, half, cols), dt),
            pltpu.VMEM((nx - 1, nz, half, cols), dt), pltpu.VMEM((ny - 1, nz, half, cols), dt),
            pltpu.VMEM((nz - 1, rows, cols), dt),
            pltpu.SemaphoreType.DMA((nz * nx * ny,)), pltpu.SemaphoreType.DMA((n,)), pltpu.SemaphoreType.DMA((n,))],
        compiler_params=pltpu.CompilerParams(collective_id=cid, has_side_effects=True, vmem_limit_bytes=60 << 20),
        name="reduce_all")
    if parts == 1:
        return one(terms)
    return jnp.concatenate([one(terms[:, :, k * cols:(k + 1) * cols]) for k in range(parts)], axis=1)


def shard_peers(ny):
    return [(0, 0, dy, dc) for dy in range(ny) for dc in range(2) if dy or dc]


def weights_kernel(w_ref, wo_ref, t_ref, wall_ref, woall_ref, tall_ref, local_sem, send, recv):
    p = Place()
    nz, nx, ny = p.nz, p.nx, p.ny
    ns = ny * 2
    e, sh = lax.axis_index("expert"), lax.axis_index("shard")
    ne = nz * nx
    me = e * ns + sh
    to_e, to_s = me % ne, me // ne
    from_e, from_s = (sh * ne + e) // ns, (sh * ne + e) % ns
    moved = jnp.logical_not(jnp.logical_and(to_e == e, to_s == sh))
    peers = [q for q in p.line_peers() if not (q[2] or q[3])] + shard_peers(ny)
    barrier = pltpu.get_barrier_semaphore()
    for q in peers:
        pl.semaphore_signal(barrier, inc=1, device_id=p.dev(*q), device_id_type=MESH)

    @pl.when(moved)
    def _():
        pl.semaphore_signal(barrier, inc=1, device_id=(from_e, from_s), device_id_type=MESH)

    pl.semaphore_wait(barrier, len(peers) + moved.astype(jnp.int32))
    s, r = Pool(send), Pool(recv)
    sent = []
    neg = lambda d, n: (n - d) % n

    def push(src, dst, to):
        cp = pltpu.make_async_remote_copy(src_ref=src, dst_ref=dst, send_sem=s.take(), recv_sem=r.take(),
            device_id=p.dev(*to), device_id_type=MESH)
        cp.start()
        sent.append(cp)
        return cp

    mixed = []
    for q in shard_peers(ny):
        _, _, y, c = p.at(*q)
        mixed.append(push(w_ref.at[y * 2 + c], wall_ref.at[me], q))
    own_w = pltpu.make_async_copy(w_ref.at[sh], wall_ref.at[me], local_sem.at[0])
    own_w.start()
    entry_send, entry_recv = s.take(), r.take()
    entry = pltpu.make_async_remote_copy(src_ref=wo_ref, dst_ref=woall_ref.at[to_e], send_sem=entry_send,
        recv_sem=entry_recv, device_id=(to_e, to_s), device_id_type=MESH)
    stay = pltpu.make_async_copy(wo_ref, woall_ref.at[e], local_sem.at[1])

    @pl.when(moved)
    def _():
        entry.start()

    @pl.when(jnp.logical_not(moved))
    def _():
        stay.start()

    own_t = pltpu.make_async_copy(t_ref, tall_ref.at[sh], local_sem.at[2])
    own_t.start()
    toks = {}
    for d in range(1, ny):
        toks[d] = push(t_ref, tall_ref.at[sh], (0, 0, d, 0))
    tail = [push(t_ref, tall_ref.at[sh], (0, 0, 0, 1))]

    def block(ref, zz, size):
        z, x, _, _ = p.at(zz, 0, 0, 0)
        return ref.at[pl.ds((z * nx + x) * size, size)]

    def spread_first(ref, size):
        lines = {}
        for d in range(1, nz):
            b = block(ref, 0, size)
            lines[d] = push(b, b, (d, 0, 0, 0))
        for d in range(1, nx):
            b = block(ref, 0, size)
            tail.append(push(b, b, (0, d, 0, 0)))
        return lines

    def spread_next(ref, size, lines, d):
        lines[d].wait_recv()
        for dx in range(1, nx):
            b = block(ref, neg(d, nz), size)
            tail.append(push(b, b, (0, dx, 0, 0)))

    own_w.wait()
    for cp in mixed:
        cp.wait_recv()
    lines_w = spread_first(wall_ref, ns)

    @pl.when(moved)
    def _():
        entry.wait()

    @pl.when(jnp.logical_not(moved))
    def _():
        stay.wait()

    lines_o = spread_first(woall_ref, 1)
    for d in range(1, ny):
        toks[d].wait_recv()
        _, _, y, c = p.at(0, 0, neg(d, ny), 0)
        b = tall_ref.at[y * 2 + c]
        tail.append(push(b, b, (0, 0, 0, 1)))
    for d in range(1, nz):
        spread_next(wall_ref, ns, lines_w, d)
    for d in range(1, nz):
        spread_next(woall_ref, 1, lines_o, d)
    for cp in tail:
        cp.wait_recv()
    for cp in sent:
        cp.wait_send()
    own_t.wait()


def gather_weights(w, wo, t, cid):
    nz, nx, ny = grid_of()
    ns, ne = ny * 2, nz * nx
    n = 2 * ns + 2 + 2 * (nz + nx + nz * nx) + 2 * ny + 8
    return pl.pallas_call(weights_kernel,
        out_shape=(jax.ShapeDtypeStruct((ne * ns,) + w.shape[1:], w.dtype),
            jax.ShapeDtypeStruct((ne,) + wo.shape, wo.dtype), jax.ShapeDtypeStruct((ns,) + t.shape, t.dtype)),
        in_specs=[VM, VM, VM], out_specs=(ANY, ANY, ANY),
        scratch_shapes=[pltpu.SemaphoreType.DMA((3,)), pltpu.SemaphoreType.DMA((n,)), pltpu.SemaphoreType.DMA((n,))],
        compiler_params=pltpu.CompilerParams(collective_id=cid, has_side_effects=True),
        name="gather_weights")(w, wo, t)


def pack_gather_kernel(t_ref, o_ref, local_sem, send, recv):
    p = Place()
    ny = p.ny
    p.greet([(0, 0, d, 0) for d in range(1, ny)] + [(0, 0, 0, 1)])
    sh = lax.axis_index("shard")
    own = pltpu.make_async_copy(t_ref, o_ref.at[sh], local_sem)
    own.start()
    s, r = Pool(send), Pool(recv)
    sent, tail, along = [], [], {}
    rows = t_ref.shape[0]
    pieces = 4

    def push(src, dst, to):
        cp = pltpu.make_async_remote_copy(src_ref=src, dst_ref=dst, send_sem=s.take(), recv_sem=r.take(),
            device_id=p.dev(*to), device_id_type=MESH)
        cp.start()
        sent.append(cp)
        return cp

    part = [pl.ds(k * (rows // pieces), rows // pieces) for k in range(pieces)]
    for k in range(pieces):
        for d in range(1, ny):
            along[k, d] = push(t_ref.at[part[k]], o_ref.at[sh, part[k]], (0, 0, d, 0))
    tail.append(push(t_ref, o_ref.at[sh], (0, 0, 0, 1)))
    for k in range(pieces):
        for d in range(1, ny):
            along[k, d].wait_recv()
            _, _, y, c = p.at(0, 0, (ny - d) % ny, 0)
            b = o_ref.at[y * 2 + c, part[k]]
            tail.append(push(b, b, (0, 0, 0, 1)))
    for cp in tail:
        cp.wait_recv()
    for cp in sent:
        cp.wait_send()
    own.wait()


def pack_gather(t, cid):
    nz, nx, ny = grid_of()
    n = 8 * ny
    return pl.pallas_call(pack_gather_kernel,
        out_shape=jax.ShapeDtypeStruct((ny * 2,) + t.shape, t.dtype), in_specs=[VM], out_specs=VM,
        scratch_shapes=[pltpu.SemaphoreType.DMA, pltpu.SemaphoreType.DMA((n,)), pltpu.SemaphoreType.DMA((n,))],
        compiler_params=pltpu.CompilerParams(collective_id=cid, has_side_effects=True),
        name="pack_gather")(t)


def pack_reduce_body(p, g_ref, out_ref, acc, rc, ry, push, pieces=4):
    ny = p.ny
    rows = g_ref.shape[1]
    step = rows // pieces
    part = [pl.ds(k * step, step) for k in range(pieces)]
    order = list(range(1, ny)) + [0]
    cores, along = {}, {}
    for k in range(pieces):
        for dy in order:
            _, _, y, c = p.at(0, 0, dy, 1)
            cores[k, dy] = push(g_ref.at[y * 2 + c, part[k]], rc.at[dy, part[k]], (0, 0, 0, 1))

    def first():
        for k in range(pieces):
            for dy in order:
                _, _, y, c = p.at(0, 0, dy, 0)
                cores[k, dy].wait_recv()
                both = g_ref[y * 2 + c, part[k], :].astype(jnp.float32) + rc[dy, part[k], :].astype(jnp.float32)
                if dy:
                    acc[dy - 1, part[k], :] = both.astype(acc.dtype)
                    along[k, dy] = push(acc.at[dy - 1, part[k]], ry.at[dy - 1, part[k]], (0, 0, dy, 0))
                else:
                    out_ref[part[k], :] = both

    def second():
        for k in range(pieces):
            for dy in range(1, ny):
                along[k, dy].wait_recv()
                out_ref[part[k], :] = out_ref[part[k], :] + ry[dy - 1, part[k], :].astype(jnp.float32)

    return first, second


def pack_reduce_kernel(g_ref, out_ref, acc, rc, ry, send, recv):
    p = Place()
    p.greet([(0, 0, d, 0) for d in range(1, p.ny)] + [(0, 0, 0, 1)])
    s, r = Pool(send), Pool(recv)
    sent = []

    def push(src, dst, to):
        cp = pltpu.make_async_remote_copy(src_ref=src, dst_ref=dst, send_sem=s.take(), recv_sem=r.take(),
            device_id=p.dev(*to), device_id_type=MESH)
        cp.start()
        sent.append(cp)
        return cp

    first, second = pack_reduce_body(p, g_ref, out_ref, acc, rc, ry, push)
    first()
    second()
    for cp in sent:
        cp.wait_send()


def pack_scratch(ny, rows, width, dt):
    return [pltpu.VMEM((ny - 1, rows, width), dt), pltpu.VMEM((ny, rows, width), dt), pltpu.VMEM((ny - 1, rows, width), dt)]


def pack_reduce(terms, cid):
    nz, nx, ny = grid_of()
    ns, rows, width = terms.shape
    n = 8 * ny
    return pl.pallas_call(pack_reduce_kernel,
        out_shape=jax.ShapeDtypeStruct((rows, width), jnp.float32), in_specs=[VM], out_specs=VM,
        scratch_shapes=pack_scratch(ny, rows, width, terms.dtype)
            + [pltpu.SemaphoreType.DMA((n,)), pltpu.SemaphoreType.DMA((n,))],
        compiler_params=pltpu.CompilerParams(collective_id=cid, has_side_effects=True, vmem_limit_bytes=40 << 20),
        name="pack_reduce")(terms)


def grads_kernel(wo_ref, w_ref, s_ref, n_ref, wo_out, w_out, s_out, n_out,
                 wo_x, wo_z, wo_l, wo_r, w_x, w_z, w_l, w_r, s_x, s_z, s_l, acc, rc, ry, load_sem, send, recv):
    p = Place()
    nz, nx, ny = p.nz, p.nx, p.ny
    ns, ne = ny * 2, nz * nx
    e, sh = lax.axis_index("expert"), lax.axis_index("shard")
    me = e * ns + sh
    own_e, own_s = (sh * ne + e) // ns, (sh * ne + e) % ns
    from_e, from_s = me % ne, me // ne
    moved = jnp.logical_not(jnp.logical_and(own_e == e, own_s == sh))
    peers = [q for q in p.line_peers() if not (q[2] or q[3])] + shard_peers(ny)
    barrier = pltpu.get_barrier_semaphore()
    for q in peers:
        pl.semaphore_signal(barrier, inc=1, device_id=p.dev(*q), device_id_type=MESH)

    @pl.when(moved)
    def _():
        pl.semaphore_signal(barrier, inc=1, device_id=(from_e, from_s), device_id_type=MESH)

    pl.semaphore_wait(barrier, len(peers) + moved.astype(jnp.int32))
    s, r = Pool(send), Pool(recv)
    sent = []

    def push(src, dst, to):
        cp = pltpu.make_async_remote_copy(src_ref=src, dst_ref=dst, send_sem=s.take(), recv_sem=r.take(),
            device_id=p.dev(*to), device_id_type=MESH)
        cp.start()
        sent.append(cp)
        return cp

    zs = list(range(1, nz)) + [0]
    jobs = [(w_ref, w_x, w_z, w_l, ns, 0), (s_ref, s_x, s_z, s_l, ns, nz), (wo_ref, wo_x, wo_z, wo_l, 1, 2 * nz)]

    def group(ref, dz, dx, size):
        z, x, _, _ = p.at(dz, dx, 0, 0)
        return ref.at[pl.ds((z * nx + x) * size, size)]

    xs, loads, lines = {}, {}, {}
    for j, (ref, x_buf, z_buf, l_buf, size, base) in enumerate(jobs):
        for dz in zs:
            for dx in range(1, nx):
                xs[j, dz, dx] = push(group(ref, dz, dx, size), x_buf.at[dx - 1, dz], (0, dx, 0, 0))
            loads[j, dz] = pltpu.make_async_copy(group(ref, dz, 0, size), l_buf.at[dz], load_sem.at[base + dz])
            loads[j, dz].start()
    first, second = pack_reduce_body(p, n_ref, n_out, acc, rc, ry, push)
    first()
    for j, (ref, x_buf, z_buf, l_buf, size, base) in enumerate(jobs):
        for dz in zs:
            loads[j, dz].wait()
            for dx in range(1, nx):
                xs[j, dz, dx].wait_recv()
            total = l_buf[dz].astype(jnp.float32)
            for dx in range(1, nx):
                total = total + x_buf[dx - 1, dz].astype(jnp.float32)
            l_buf[dz] = total.astype(l_buf.dtype)
            if dz:
                lines[j, dz] = push(l_buf.at[dz], z_buf.at[dz - 1], (dz, 0, 0, 0))
    second()
    last = []
    entry = pltpu.make_async_remote_copy(src_ref=wo_l.at[0, 0], dst_ref=wo_r, send_sem=s.take(),
        recv_sem=r.take(), device_id=(own_e, own_s), device_id_type=MESH)
    for j, (ref, x_buf, z_buf, l_buf, size, base) in enumerate(jobs):
        total = l_buf[0].astype(jnp.float32)
        for d in range(1, nz):
            lines[j, d].wait_recv()
            total = total + z_buf[d - 1].astype(jnp.float32)
        l_buf[0] = total.astype(l_buf.dtype)
        if j == 0:
            for q in shard_peers(ny):
                _, _, y, c = p.at(*q)
                last.append(push(l_buf.at[0, y * 2 + c], w_r.at[sh], q))
            w_r[sh] = l_buf[0, sh]
        elif j == 1:
            for q in shard_peers(ny):
                _, _, y, c = p.at(*q)
                last.append(push(l_buf.at[0, y * 2 + c], s_out.at[sh], q))
            s_out[sh] = l_buf[0, sh]

    @pl.when(moved)
    def _():
        entry.start()

    for cp in last:
        cp.wait_recv()
    w_out[...] = w_r[...].astype(jnp.float32)

    @pl.when(moved)
    def _():
        entry.wait()
        wo_out[...] = wo_r[...].astype(jnp.float32)

    @pl.when(jnp.logical_not(moved))
    def _():
        wo_out[...] = wo_l[0, 0].astype(jnp.float32)

    for cp in sent:
        cp.wait_send()


def reduce_grads(wo, w, small, inp, cid):
    nz, nx, ny = grid_of()
    ns, ne = ny * 2, nz * nx
    bf, f32 = jnp.bfloat16, jnp.float32
    rows_o, width = wo.shape[1:]
    rows_w, cb = w.shape[1:]
    rows_n = inp.shape[1]
    n = 3 * nz * nx + 3 * nz + 2 * ns + 8 * ny + 8
    small_block = small.shape[1:]
    return pl.pallas_call(grads_kernel,
        out_shape=(jax.ShapeDtypeStruct((rows_o, width), f32), jax.ShapeDtypeStruct((ns, rows_w, cb), f32),
            jax.ShapeDtypeStruct((ns,) + small_block, f32), jax.ShapeDtypeStruct((rows_n, width), f32)),
        in_specs=[ANY, ANY, ANY, VM], out_specs=(VM, VM, VM, VM),
        scratch_shapes=[pltpu.VMEM((nx - 1, nz, 1, rows_o, width), bf), pltpu.VMEM((nz - 1, 1, rows_o, width), bf),
            pltpu.VMEM((nz, 1, rows_o, width), bf), pltpu.VMEM((rows_o, width), bf),
            pltpu.VMEM((nx - 1, nz, ns, rows_w, cb), bf), pltpu.VMEM((nz - 1, ns, rows_w, cb), bf),
            pltpu.VMEM((nz, ns, rows_w, cb), bf), pltpu.VMEM((ns, rows_w, cb), bf),
            pltpu.VMEM((nx - 1, nz, ns) + small_block, f32), pltpu.VMEM((nz - 1, ns) + small_block, f32),
            pltpu.VMEM((nz, ns) + small_block, f32)]
            + pack_scratch(ny, rows_n, width, bf)
            + [pltpu.SemaphoreType.DMA((3 * nz,)), pltpu.SemaphoreType.DMA((n,)), pltpu.SemaphoreType.DMA((n,))],
        compiler_params=pltpu.CompilerParams(collective_id=cid, has_side_effects=True, vmem_limit_bytes=56 << 20),
        name="reduce_grads")(wo, w, small, inp)


QUERY_HEADS = 32
KEY_VALUE_HEADS = 4
HEAD = 128
EPSILON = 1e-06
THETA = 1000000.0


def norm_rows(values_in, gain):
    return values_in * lax.rsqrt(jnp.mean(values_in * values_in, axis=-1, keepdims=True) + EPSILON) * gain


def rotate(vectors, position):
    half_size = vectors.shape[-1] // 2
    freqs = jnp.exp(jnp.arange(half_size, dtype=jnp.float32) * (-2.0 * math.log(THETA) / vectors.shape[-1]))
    angles = position[:, None] * freqs[None, :]
    cosine = jnp.cos(angles)[:, None, :]
    sine = jnp.sin(angles)[:, None, :]
    first = vectors[..., :half_size]
    second = vectors[..., half_size:]
    return jnp.concatenate([first * cosine - second * sine, second * cosine + first * sine], axis=-1)


def segment_starts(segment):
    index = jnp.arange(segment.shape[0], dtype=jnp.int32)
    same = segment[:, None] == segment[None, :]
    return jnp.min(jnp.where(same, index[None, :], segment.shape[0]), axis=1)


def shards(tokens_in, out_grad, segment_ids, expert_ids, route_weights, attn_gain, qkv_weight, q_gain, k_gain,
           out_weight, moe_gain, expert_in, expert_out):
    f32, bf = jnp.float32, jnp.bfloat16
    n_expert, n_shard = lax.axis_size("expert"), lax.axis_size("shard")
    nd = n_expert * n_shard
    rows, width = tokens_in.shape
    me = lax.axis_index("expert") * n_shard + lax.axis_index("shard")
    shard = lax.axis_index("shard")
    heads = QUERY_HEADS // n_shard
    group = QUERY_HEADS // KEY_VALUE_HEADS
    kv_heads = max(1, KEY_VALUE_HEADS // n_shard)
    copies = max(1, n_shard // KEY_VALUE_HEADS)
    per = heads // kv_heads
    q_cols, kv_cols = heads * HEAD, kv_heads * HEAD
    q_all, kv_all = QUERY_HEADS * HEAD, KEY_VALUE_HEADS * HEAD
    wide = qkv_weight.shape[0]

    scaled = (qkv_weight.astype(f32) * attn_gain.astype(f32)[:, None]).astype(bf)

    def by_shard(part, cols, count):
        part = part.reshape(wide, n_shard // count, 1, cols)
        return jnp.broadcast_to(part, (wide, n_shard // count, count, cols)).reshape(wide, n_shard, cols)

    pieces = jnp.concatenate([by_shard(scaled[:, :q_all], q_cols, 1),
        by_shard(scaled[:, q_all:q_all + kv_all], kv_cols, copies),
        by_shard(scaled[:, q_all + kv_all:], kv_cols, copies)], axis=2).transpose(1, 0, 2)
    weights, out_rows, pack = gather_weights(pieces, out_weight, tokens_in, 0)
    weights = weights.reshape(width, -1)
    out_rows = out_rows.reshape(heads * HEAD, width)
    pack = pack.reshape(n_shard * rows, width)
    length = pack.shape[0]

    high = route_weights.astype(bf)
    rest = route_weights - high.astype(f32)
    middle = rest.astype(bf)
    low = (rest - middle.astype(f32)).astype(bf)
    top = expert_ids.shape[1]
    gains = jnp.zeros((rows,), bf)
    at = 0
    for g in (moe_gain, q_gain, k_gain):
        gains = lax.dynamic_update_slice(gains, g, (at,))
        at += g.shape[0]
    extra = jnp.concatenate([expert_ids.astype(bf), high, middle, low, gains[:, None]], axis=1)
    extra = jnp.pad(extra, ((0, 0), (0, 128 - extra.shape[1])))
    grads_all = gather_all(jnp.concatenate([out_grad, extra], axis=1), 1)
    info = grads_all[:, :, width:].astype(f32)
    ids_all = info[:, :, :top]
    weights_all = info[:, :, top:2 * top] + info[:, :, 2 * top:3 * top] + info[:, :, 3 * top:4 * top]
    gain_col = info[:, :, 4 * top]
    g0, g1, g2 = moe_gain.shape[0], q_gain.shape[0], k_gain.shape[0]
    moe_scale = gain_col[:, :g0].reshape(-1)
    query_gain = gain_col[:, g0:g0 + g1].reshape(-1)
    key_gain = gain_col[:, g0 + g1:g0 + g1 + g2].reshape(-1)

    pack_f32 = pack.astype(f32)
    inverse = lax.rsqrt(jnp.mean(pack_f32 * pack_f32, axis=-1, keepdims=True) + EPSILON)
    projected = jnp.dot(pack, weights, preferred_element_type=f32) * inverse
    segment = segment_ids[0]
    index = jnp.arange(length, dtype=jnp.int32)
    position = (index - segment_starts(segment)).astype(f32)
    query_raw = projected[:, :q_cols].reshape(length, heads, HEAD)
    key_raw = projected[:, q_cols:q_cols + kv_cols].reshape(length, kv_heads, HEAD)
    values = projected[:, q_cols + kv_cols:].astype(bf).reshape(length, kv_heads, HEAD)

    def prepare(query_in, key_in, gain_q, gain_k):
        return rotate(norm_rows(query_in, gain_q), position), rotate(norm_rows(key_in, gain_k), position)

    (query_rot, key_rot), prepare_back = jax.vjp(prepare, query_raw, key_raw, query_gain, key_gain)
    queries = query_rot.astype(bf).reshape(length, kv_heads, per, HEAD)
    keys = key_rot.astype(bf)
    allowed = (segment[:, None] == segment[None, :]) & (index[None, :] <= index[:, None])
    factor = HEAD ** (-0.5)
    scores = jnp.einsum("tkgd,skd->kgts", queries, keys, preferred_element_type=f32) * factor
    scores = jnp.where(allowed[None, None], scores, -1e30)
    highest = jnp.max(scores, axis=-1, keepdims=True)
    log_total = highest + jnp.log(jnp.sum(jnp.exp(scores - highest), axis=-1, keepdims=True))
    probs = jnp.exp(scores - log_total)
    probs_low = probs.astype(bf)
    attn = jnp.einsum("kgts,skd->tkgd", probs_low, values, preferred_element_type=f32).astype(bf)
    attn_flat = attn.reshape(length, q_cols)
    mixed = jnp.dot(attn_flat, out_rows, preferred_element_type=f32).astype(bf)
    hidden_state = tokens_in.astype(f32) + pack_reduce(mixed.reshape(n_shard, rows, width), 2)
    hidden_inverse = lax.rsqrt(jnp.mean(hidden_state * hidden_state, axis=-1, keepdims=True) + EPSILON)
    hidden_norm = hidden_state * hidden_inverse
    moe_in = (hidden_norm * moe_scale).astype(bf)

    rows_all = gather_all(moe_in, 3)
    cap = max(2, 2 * rows * top // nd)
    hit = ids_all == me.astype(f32)
    any_hit = jnp.any(hit, axis=-1)
    gate = jnp.sum(jnp.where(hit, weights_all, 0.0), axis=-1)
    lower = (jnp.arange(rows)[:, None] <= jnp.arange(rows)[None, :]).astype(bf)
    rank = jnp.dot(any_hit.astype(bf), lower, preferred_element_type=f32) - 1.0
    chosen = (jnp.arange(cap, dtype=f32)[None, :, None] == rank[:, None, :]) & any_hit[:, None, :]
    slot_gate = jnp.sum(jnp.where(chosen, gate[:, None, :], 0.0), axis=-1)
    select = chosen.astype(bf)
    in_rows = jnp.einsum("bkt,btd->bkd", select, rows_all, preferred_element_type=f32).astype(bf).reshape(nd * cap, width)
    grad_rows = (jnp.einsum("bkt,btd->bkd", select, grads_all[:, :, :width], preferred_element_type=f32)
        * slot_gate[:, :, None]).astype(bf).reshape(nd * cap, width)
    w_in, w_out = expert_in[0], expert_out[0]
    size = w_out.shape[0]
    pre = jnp.dot(in_rows, w_in, preferred_element_type=f32)
    gate_part, up_part = pre[:, :size], pre[:, size:]
    sigma = jax.nn.sigmoid(gate_part)
    active = gate_part * sigma
    hidden = (active * up_part).astype(bf)
    outputs = jnp.dot(hidden, w_out, preferred_element_type=f32).astype(bf)
    weighted = (outputs.astype(f32) * slot_gate.reshape(-1, 1)).astype(bf).reshape(nd, cap, width)
    out_terms = jnp.einsum("bkt,bkd->btd", select, weighted, preferred_element_type=f32).astype(bf)
    moe_sum = reduce_all(out_terms, f32, 4)
    hidden_grad = jnp.einsum("rd,fd->rf", grad_rows, w_out, preferred_element_type=f32)
    gate_grad = hidden_grad * up_part * (sigma * (1.0 + gate_part * (1.0 - sigma)))
    pre_grad = jnp.concatenate([gate_grad, hidden_grad * active], axis=-1).astype(bf)
    rows_grad = jnp.einsum("rc,dc->rd", pre_grad, w_in, preferred_element_type=f32).astype(bf).reshape(nd, cap, width)
    grad_terms = jnp.einsum("bkt,bkd->btd", select, rows_grad, preferred_element_type=f32).astype(bf)
    moe_grad = reduce_all(grad_terms, f32, 5)
    expert_in_grad = jnp.einsum("rd,rc->dc", in_rows, pre_grad, preferred_element_type=f32)[None]
    expert_out_grad = jnp.einsum("rf,rd->fd", hidden, grad_rows, preferred_element_type=f32)[None]
    block_output = (hidden_state + moe_sum).astype(bf)

    scaled_grad = moe_grad * moe_scale
    moe_gain_grad = jnp.sum(moe_grad * hidden_norm, axis=0)
    residual = out_grad.astype(f32) + hidden_inverse * (
        scaled_grad - hidden_norm * jnp.mean(scaled_grad * hidden_norm, axis=-1, keepdims=True))
    residual_pack = pack_gather(residual.astype(bf), 6).reshape(length, width)
    out_term = jnp.einsum("tc,td->cd", attn_flat, residual_pack, preferred_element_type=f32).astype(bf)
    attn_grad = jnp.einsum("td,cd->tc", residual_pack, out_rows, preferred_element_type=f32).astype(bf)
    attn_grad = attn_grad.reshape(length, kv_heads, per, HEAD)
    delta = jnp.einsum("tkgd,tkgd->kgt", attn_grad, attn, preferred_element_type=f32)
    prob_grad = jnp.einsum("tkgd,skd->kgts", attn_grad, values, preferred_element_type=f32)
    score_grad = (probs * (prob_grad - delta[..., None])).astype(bf)
    query_grad = jnp.einsum("kgts,skd->tkgd", score_grad, keys, preferred_element_type=f32) * factor
    key_grad = jnp.einsum("kgts,tkgd->skd", score_grad, queries, preferred_element_type=f32) * factor
    value_grad = jnp.einsum("kgts,tkgd->skd", probs_low, attn_grad, preferred_element_type=f32)
    query_back, key_back, query_gain_grad, key_gain_grad = prepare_back((query_grad.reshape(length, heads, HEAD), key_grad))
    projected_grad = jnp.concatenate([query_back.reshape(length, -1), key_back.reshape(length, -1),
        value_grad.reshape(length, -1)], axis=1)
    projected_grad = (projected_grad * inverse).astype(bf)
    qkv_term = jnp.einsum("td,tc->dc", pack, projected_grad, preferred_element_type=f32).astype(bf)
    input_term = jnp.einsum("tc,dc->td", projected_grad, weights, preferred_element_type=f32).astype(bf)

    def lanes(v):
        v = v.reshape(nd, -1)
        return jnp.pad(v, ((0, 0), (0, 128 - v.shape[1])))[:, None]

    small = jnp.concatenate([lanes(moe_gain_grad), lanes(query_gain_grad), lanes(key_gain_grad),
        jnp.zeros((nd, 5, 128), f32)], axis=1)
    out_weight_grad, qkv_part, small_sum, input_sum = reduce_grads(out_term.reshape(n_expert, -1, width),
        qkv_term.reshape(nd, wide, -1), small, input_term.reshape(n_shard, rows, width), 7)
    small_sum = jnp.sum(small_sum, axis=0)

    def whole_cols(part, count):
        part = part.transpose(1, 0, 2).reshape(wide, n_shard // count, count, -1)
        return jnp.sum(part, axis=2).reshape(wide, -1)

    raw = jnp.concatenate([whole_cols(qkv_part[:, :, :q_cols], 1), whole_cols(qkv_part[:, :, q_cols:q_cols + kv_cols], copies),
        whole_cols(qkv_part[:, :, q_cols + kv_cols:], copies)], axis=1)
    attn_gain_grad = jnp.sum(raw * qkv_weight.astype(f32), axis=1)
    qkv_weight_grad = raw * attn_gain.astype(f32)[:, None]
    own = tokens_in.astype(f32)
    own_norm = own * lax.rsqrt(jnp.mean(own * own, axis=-1, keepdims=True) + EPSILON)
    input_grad = (residual + input_sum - own_norm * jnp.mean(input_sum * own_norm, axis=-1, keepdims=True)).astype(bf)
    return (block_output, input_grad, attn_gain_grad, qkv_weight_grad, small_sum[1, :g1], small_sum[2, :g2],
        out_weight_grad, small_sum[0, :g0], expert_in_grad, expert_out_grad)


def solution(mesh):
    both = ("expert", "shard")
    row, rows2, rows3 = P(both), P(both, None), P(both, None, None)
    return jax.shard_map(
        shards, mesh=mesh,
        in_specs=(rows2, rows2, P("expert", None), rows2, rows2, row, rows2, row, row, rows2, row, rows3, rows3),
        out_specs=(rows2, rows2, row, rows2, row, row, rows2, row, rows3, rows3),
        check_vma=False,
    )
```

time: 2180 us -> 1020 us (0.47)
  waiting for transfers between devices: 1370 us -> 0 us
  Pallas kernels: 0 us -> 720 us
  local copies, waits for them, and re-layouts: 286 us -> 31 us
  other arithmetic: 184 us -> 56.3 us
  blocking collectives: 93.8 us -> 0 us
  starting transfers between devices: 29.5 us -> 0 us
    pallas_call x0 -> x8, Pallas kernels: none -> 720 us  [the longest x2 189 us: reduce_all(): return one(terms)]
    reduce_scatter x2 -> x0, waiting for transfers between devices: 678 us -> none  [the longest x1 447 us: shards(): lax.psum_scatter(qkv_term, ('expert', 'shard'), scatter_dimension=0, tile...]
    all_to_all x4 -> x0, waiting for transfers between devices: 531 us -> none  [the longest x1 170 us: shards(): lax.all_to_all(send_rows, ('expert', 'shard'), split_axis=0, concat_axis=...]
    all_gather x3 -> x0, waiting for transfers between devices: 159 us -> none  [the longest x1 87.9 us: shards(): lax.all_gather(qkv_weight, ('expert', 'shard'), axis=0, tiled=True)]
    unnamed x170 -> x146, local copies, waits for them, and re-layouts: 152 us -> 18.7 us
    unnamed x3 -> x6, other arithmetic: 104 us -> 1.57 us
    unnamed x2 -> x0, blocking collectives: 93.8 us -> none
    broadcast_in_dim x2, local copies, waits for them, and re-layouts: 63.8 us -> 0.01 us  [the longest x1 0.01 us: shards(): gains[:, None]]
  transfers between devices with their start and end apart: 10 -> 0, of which waited for: 8 -> 0; matrix products, arithmetic and copies ran while one was open for 17% -> 0% of each run, Pallas kernels for 0% -> 0%
where the time goes in v1:
time: 1020 us; the launch traced here: 1000 us
  Pallas kernels  720 us (71%)
  matrix products  195 us (19%)
  other arithmetic  56.3 us (6%)
  local copies, waits for them, and re-layouts  31 us (3%)
    pallas_call x2, Pallas kernels, reduce_all(): return one(terms)  189 us
    pallas_call x2, Pallas kernels, gather_all(): pl.pallas_call(gather_all_kernel, out_shape=jax.ShapeDtypeStruct((nz * nx...  188 us
    pallas_call x1, Pallas kernels, gather_weights(): pl.pallas_call(weights_kernel, out_shape=(jax.ShapeDtypeStruct((ne * ns,)...  159 us
    pallas_call x1, Pallas kernels, reduce_grads(): pl.pallas_call(grads_kernel, out_shape=(jax.ShapeDtypeStruct((rows_o, wid...  150 us

profile of v1, /device:TPU:2, one launch (start us, length us, event | category | flops | bytes accessed | tf_op | source)
XLA Modules:
  0.0 1003.8 jit_solution(14841692737822825568)
XLA Ops:
  3.9 158.9 %gather_weights.1 = (bf16[32,64,1280]{2,1,0:T(8,128)(2,1)}, bf16[8,128,2048]{2,1,0:T(8,128)(2,1)}, bf16[4,128,2048]{2,1,0:T(8,128)(2,1)}) custom-call(bf16[4,64,1280]{2,1,0:T(8,128)(2,1)} %maximum_bitcast_fusion.w_ref, bf16[128,2048]{1,0:T(8,128)(2,1)} %wo_ref.1, bf16[128,2048]{1,0:T(8,128)(2,1)} %t_ref.1), custom_call_target="tpu_custom_call" | custom-call | tf_op jit(solution)/shard_map/gather_weights/pallas_call | solution.py:356
  162.8 2.1 multiply_reduce_fusion
  165.5 6.0 convolution_multiply_fusion
  171.5 1.9 slice_bitcast_fusion.1
  175.5 1.9 fusion.42.b_ref
  177.4 94.2 %gather_all.2 = bf16[32,128,2176]{2,1,0:T(8,128)(2,1)} custom-call(bf16[128,2176]{1,0:T(8,128)(2,1)} %fusion.42.b_ref), custom_call_target="tpu_custom_call" | custom-call | tf_op jit(solution)/shard_map/gather_all/pallas_call | solution.py:125
  275.9 1.9 fusion.22
  279.1 2.1 subtract_convert_fusion
  285.3 3.9 fusion.9
  294.4 2.0 convolution_convert_fusion.8
  296.4 2.1 copy-done.60
  298.5 2.4 convolution_convert_fusion.6
  301.0 15.9 %pack_reduce.1 = f32[128,2048]{1,0:T(8,128)S(1)} custom-call(bf16[4,128,2048]{2,1,0:T(8,128)(2,1)S(1)} %bitcast.226), custom_call_target="tpu_custom_call" | custom-call | tf_op jit(solution)/shard_map/pack_reduce/pallas_call | solution.py:473
  318.7 2.2 multiply_convert_fusion.5.b_ref
  320.9 93.8 %gather_all.3 = bf16[32,128,2048]{2,1,0:T(8,128)(2,1)} custom-call(bf16[128,2048]{1,0:T(8,128)(2,1)} %multiply_convert_fusion.5.b_ref), custom_call_target="tpu_custom_call" | custom-call | tf_op jit(solution)/shard_map/gather_all/pallas_call | solution.py:125
  414.7 2.2 fusion.85
  417.1 11.9 %convolution_convert_fusion.4 = bf16[32,64,2048]{2,1,0:T(8,128)(2,1)} fusion(bf16[32,128,2048]{2,1,0:T(8,128)(2,1)} %gather_all.3, f32[32,128]{1,0:T(8,128)S(1)} %convolution_add_fusion, pred[32,128]{1,0:T(8,128)(4,1)S(1)} %get-tuple-element.32), kind=kOutput, calls=%fused_computation.26 | convolution fusion | flops 1078460416 | bytes 25186304 | tf_op jit(solution)/shard_map/bkt,btd->bkd/dot_general | solution.py:729
  428.9 19.1 %fusion.6 = f32[2048,1536]{0,1:T(8,128)} fusion(bf16[2048,2048]{1,0:T(8,128)(2,1)} %bitcast.229, bf16[1,2048,1536]{2,1,0:T(8,128)(2,1)} %param.24), kind=kOutput, calls=%fused_computation.18 | convolution fusion | flops 12884901888 | bytes 27262976 | tf_op jit(solution)/shard_map/dot_general | solution.py:734
  448.1 2.3 fusion.21
  450.7 9.5 multiply_convert_fusion
  460.2 16.1 %multiply_convert_fusion.3 = (bf16[2048,768]{0,1:T(8,128)(2,1)}, bf16[2048,768]{0,1:T(8,128)(2,1)}, bf16[2048,768]{0,1:T(8,128)(2,1)S(1)}) fusion(f32[2048,1536]{0,1:T(8,128)} %fusion.6, bf16[2048,2048]{1,0:T(8,128)(2,1)} %bitcast.233, bf16[1,768,2048]{2,1,0:T(8,128)(2,1)S(1)} %copy-done), kind=kOutput, calls=%fused_computation.21 | convolution fusion | flops 6466043904 | bytes 33554432 | tf_op jit(solution)/shard_map/rd,fd->rf/dot_general | solution.py:743
  476.3 11.9 %convolution_bitcast_fusion.1 = f32[1,768,2048]{2,1,0:T(8,128)} fusion(bf16[2048,768]{0,1:T(8,128)(2,1)S(1)} %get-tuple-element.36, bf16[2048,2048]{1,0:T(8,128)(2,1)} %bitcast.234), kind=kOutput, calls=%fused_computation.30 | convolution fusion | flops 6442450944 | bytes 17825792 | tf_op jit(solution)/shard_map/rf,rd->fd/dot_general | solution.py:750
  488.3 17.1 %convolution_bitcast_fusion = f32[1,2048,1536]{2,1,0:T(8,128)} fusion(bf16[2048,2048]{1,0:T(8,128)(2,1)S(1)} %bitcast.232, bf16[2048,768]{0,1:T(8,128)(2,1)S(1)} %copy-done.65, bf16[2048,768]{0,1:T(8,128)(2,1)S(1)} %copy-done.63), kind=kOutput, calls=%fused_computation.6 | convolution fusion | flops 12897484800 | bytes 27262976 | tf_op jit(solution)/shard_map/rd,rc->dc/dot_general | solution.py:749
  505.4 19.2 %convolution_convert_fusion.3 = bf16[2048,2048]{1,0:T(8,128)(2,1)} fusion(bf16[1,2048,1536]{2,1,0:T(8,128)(2,1)} %param.24, bf16[2048,768]{0,1:T(8,128)(2,1)} %get-tuple-element.35, bf16[2048,768]{0,1:T(8,128)(2,1)S(1)} %copy-done.64), kind=kOutput, calls=%fused_computation.14 | convolution fusion | flops 12901679104 | bytes 20971520 | tf_op jit(solution)/shard_map/rc,dc->rd/dot_general | solution.py:746
  524.6 13.7 %convolution_convert_fusion.g_ref = bf16[32,128,2048]{2,1,0:T(8,128)(2,1)} fusion(bf16[32,64,2048]{2,1,0:T(8,128)(2,1)} %bitcast.228, f32[32,128]{1,0:T(8,128)S(1)} %convolution_add_fusion, pred[32,128]{1,0:T(8,128)(4,1)S(1)} %get-tuple-element.32), kind=kOutput, calls=%fused_computation.4 | convolution fusion | flops 1082654720 | bytes 25186304 | tf_op jit(solution)/shard_map/bkt,bkd->btd/dot_general | solution.py:747
  538.2 100.1 %reduce_all.3 = f32[128,2048]{1,0:T(8,128)} custom-call(bf16[32,128,2048]{2,1,0:T(8,128)(2,1)} %convolution_convert_fusion.g_ref), custom_call_target="tpu_custom_call" | custom-call | tf_op jit(solution)/shard_map/reduce_all/pallas_call | solution.py:237
  638.4 1.9 multiply_reduce_fusion.4
  640.3 2.7 fusion.82.t_ref
  643.0 17.7 %pack_gather.1 = bf16[4,128,2048]{2,1,0:T(8,128)(2,1)} custom-call(bf16[128,2048]{1,0:T(8,128)(2,1)} %fusion.82.t_ref), custom_call_target="tpu_custom_call" | custom-call | tf_op jit(solution)/shard_map/pack_gather/pallas_call | solution.py:405
  660.7 5.2 convolution_convert_fusion.9
  669.4 3.0 copy.155
  672.4 2.3 multiply_reduce_fusion.1
  674.8 5.1 fusion.11
  679.9 1.8 multiply_bitcast_fusion
  683.3 1.8 multiply_reduce_fusion.2
  685.2 3.0 copy_bitcast_fusion
  693.4 8.4 copy.143
  701.9 4.4 convolution_bitcast_fusion.3
  706.3 6.9 convolution_convert_fusion.7
  714.4 7.8 convolution_convert_fusion.2
  722.2 4.4 convolution_convert_fusion.5
  726.5 150.3 %reduce_grads.1 = (f32[128,2048]{1,0:T(8,128)}, f32[4,64,1280]{2,1,0:T(8,128)}, f32[4,8,128]{2,1,0:T(8,128)}, f32[128,2048]{1,0:T(8,128)}) custom-call(bf16[8,128,2048]{2,1,0:T(8,128)(2,1)} %bitcast.241, bf16[32,64,1280]{2,1,0:T(8,128)(2,1)} %bitcast.237, f32[32,8,128]{2,1,0:T(8,128)} %maximum_maximum_fusion.s_ref, bf16[4,128,2048]{2,1,0:T(8,128)(2,1)} %bitcast.248), custom_call_target="tpu_custom_call" | custom-call | tf_op jit(solution)/shard_map/reduce_grads/pallas_call | solution.py:589
  879.4 1.9 broadcast_multiply_fusion
  881.4 11.1 %multiply_convert_fusion.1 = bf16[2048,2048]{1,0:T(8,128)(2,1)} fusion(f32[2048]{0:T(1024)S(1)} %mul.490, bf16[2048,768]{0,1:T(8,128)(2,1)} %copy-done.62, bf16[1,768,2048]{2,1,0:T(8,128)(2,1)S(1)} %copy-done), kind=kOutput, calls=%fused_computation.3 | convolution fusion | flops 6459228160 | bytes 14688256 | tf_op jit(solution)/shard_map/dot_general | solution.py:739
  892.5 13.7 %convolution_convert_fusion.1.g_ref = bf16[32,128,2048]{2,1,0:T(8,128)(2,1)} fusion(bf16[32,64,2048]{2,1,0:T(8,128)(2,1)} %bitcast.227, f32[32,128]{1,0:T(8,128)S(1)} %convolution_add_fusion, pred[32,128]{1,0:T(8,128)(4,1)S(1)} %get-tuple-element.32), kind=kOutput, calls=%fused_computation.5 | convolution fusion | flops 1082654720 | bytes 25186304 | tf_op jit(solution)/shard_map/bkt,bkd->btd/dot_general | solution.py:741
  906.2 88.9 %reduce_all.2 = f32[128,2048]{1,0:T(8,128)} custom-call(bf16[32,128,2048]{2,1,0:T(8,128)(2,1)} %convolution_convert_fusion.1.g_ref), custom_call_target="tpu_custom_call" | custom-call | tf_op jit(solution)/shard_map/reduce_all/pallas_call | solution.py:237
  996.6 3.7 fusion.32
  1001.3 2.3 copy.203
  (211 shorter events, 39.2 us)
Async XLA Ops:
  0.6 459.6 %copy-start = (bf16[1,768,2048]{2,1,0:T(8,128)(2,1)S(1)}, bf16[1,768,2048]{2,1,0:T(8,128)(2,1)}, u32[]{:S(2)}) copy-start(bf16[1,768,2048]{2,1,0:T(8,128)(2,1)} %param.25) | copy-start | bytes 9437188
  171.5 2.1 copy-start.12
  174.8 96.9 %copy-start.33 = (f32[512,8]{0,1:T(8,128)}, f32[512,8]{0,1:T(8,128)S(1)}, u32[]{:S(2)}) copy-start(f32[512,8]{0,1:T(8,128)S(1)} %copy.129) | copy-start | bytes 49156
  174.8 101.1 %copy-start.30 = (f32[512,8]{0,1:T(8,128)}, f32[512,8]{0,1:T(8,128)S(1)}, u32[]{:S(2)}) copy-start(f32[512,8]{0,1:T(8,128)S(1)} %fusion.74) | copy-start | bytes 49156
  274.5 3.3 copy-start.42
  275.8 5.4 copy-start.48
  278.0 5.5 copy-start.38
  278.1 5.5 copy-start.50
  279.1 2.1 copy-start.18
  279.1 2.1 copy-start.20
  282.3 6.9 copy-start.43
  282.3 6.8 copy-start.40
  282.4 6.7 copy-start.46
  285.0 4.2 copy-start.24
  285.0 4.2 copy-start.26
  285.2 5.8 copy-start.13
  289.2 3.3 copy-start.1
  294.4 6.6 copy-start.4
  294.4 4.2 copy-start.60
  296.4 4.6 copy-start.15
  301.0 15.9 %copy-start.9 = (bf16[128,2048]{1,0:T(8,128)(2,1)S(1)}, bf16[128,2048]{1,0:T(8,128)(2,1)}, u32[]{:S(2)}) copy-start(bf16[128,2048]{1,0:T(8,128)(2,1)} %t_ref.1) | copy-start | bytes 1572868
  428.9 19.1 %copy-start.3 = (f32[32,128,128]{2,1,0:T(8,128)S(1)}, f32[32,128,128]{2,1,0:T(8,128)}, u32[]{:S(2)}) copy-start(f32[32,128,128]{2,1,0:T(8,128)} %copy-done.2) | copy-start | bytes 6291460
  450.7 37.5 %slice-start = ((s8[8388608]{0:T(1024)(128)(4,1)}), s8[4194304]{0:T(1024)(128)(4,1)S(1)}, s32[]{:S(2)}) async-start(s8[8388608]{0:T(1024)(128)(4,1)} %bitcast.230), calls=%async_computation | async-start | bytes 8388608
  460.2 28.0 %slice-start.1 = ((s8[8388608]{0:T(1024)(128)(4,1)}), s8[4194304]{0:T(1024)(128)(4,1)S(1)}, s32[]{:S(2)}) async-start(s8[8388608]{0:T(1024)(128)(4,1)} %bitcast.230), calls=%async_computation.1 | async-start | bytes 8388608
  476.3 11.9 %copy-start.62 = (bf16[2048,768]{0,1:T(8,128)(2,1)}, bf16[2048,768]{0,1:T(8,128)(2,1)S(1)}, u32[]{:S(2)}) copy-start(bf16[2048,768]{0,1:T(8,128)(2,1)S(1)} %get-tuple-element.36) | copy-start | bytes 9437188
  476.3 11.9 %copy-start.63 = (bf16[2048,768]{0,1:T(8,128)(2,1)S(1)}, bf16[2048,768]{0,1:T(8,128)(2,1)}, u32[]{:S(2)}) copy-start(bf16[2048,768]{0,1:T(8,128)(2,1)} %get-tuple-element.34) | copy-start | bytes 9437188
  476.3 11.9 %copy-start.65 = (bf16[2048,768]{0,1:T(8,128)(2,1)S(1)}, bf16[2048,768]{0,1:T(8,128)(2,1)}, u32[]{:S(2)}) copy-start(bf16[2048,768]{0,1:T(8,128)(2,1)} %get-tuple-element.35) | copy-start | bytes 9437188
  488.2 17.2 %copy-start.64 = (bf16[2048,768]{0,1:T(8,128)(2,1)S(1)}, bf16[2048,768]{0,1:T(8,128)(2,1)}, u32[]{:S(2)}) copy-start(bf16[2048,768]{0,1:T(8,128)(2,1)} %get-tuple-element.34) | copy-start | bytes 9437188
  538.2 102.1 %copy-start.11 = (bf16[128,2048]{1,0:T(8,128)(2,1)S(1)}, bf16[128,2048]{1,0:T(8,128)(2,1)}, u32[]{:S(2)}) copy-start(bf16[128,2048]{1,0:T(8,128)(2,1)} %param.14) | copy-start | bytes 1572868
  669.4 5.3 copy-start.14
  669.4 5.3 copy-start.36
  672.4 2.3 copy-start.29
  674.7 5.1 copy-start.25
  674.7 5.1 copy-start.27
  679.8 1.9 copy-start.19
  685.2 3.1 copy-start.7
  685.2 3.1 copy-start.8
  688.3 2.6 copy-start.41
  688.3 2.6 copy-start.47
  688.3 3.9 copy-start.44
  701.9 4.4 copy-start.23
  701.9 4.4 copy-start.56
  706.3 6.9 copy-start.32
  714.4 7.8 copy-start.16
  714.4 7.8 copy-start.22
  906.2 88.9 %copy-start.57 = (f32[128]{0:T(128)S(1)}, f32[128]{0:T(128)}, u32[]{:S(2)}) copy-start(f32[128]{0:T(128)} %get-tuple-element.51) | copy-start | bytes 1540
  906.2 88.9 %copy-start.10 = (bf16[128,2048]{1,0:T(8,128)(2,1)S(1)}, bf16[128,2048]{1,0:T(8,128)(2,1)}, u32[]{:S(2)}) copy-start(bf16[128,2048]{1,0:T(8,128)(2,1)} %t_ref.1) | copy-start | bytes 1572868
  996.6 3.7 copy-start.45
  (20 other events, 27.6 us)

commit v2 on v1

--- a/solution.py
+++ b/solution.py
@@ -1,3 +1,4 @@
+import functools
 import math
 import jax, jax.numpy as jnp
 from jax import lax
@@ -48,133 +49,57 @@
         self.used += 1
         return self.sems.at[self.used - 1]
 
-def gather_all_kernel(b_ref, o_ref, local_sem, send, recv):
+def n_sems(nz, nx, ny):
+    return (nz - 1) + nz * (nx - 1 + ny - 1 + 1) + nz * (nx * (ny - 1) + ny * (nx - 1)) + nz * (nx - 1 + ny - 1) + nz * (nx * (ny - 1) + ny * (nx - 1))
+
+def reduce_rows_kernel(g_ref, selt_ref, out_ref, give, acc, rc, ra1, rb1, ra2, rb2, rz, send, recv):
     p = Place()
     nz, nx, ny = p.nz, p.nx, p.ny
-    half = b_ref.shape[0] // 2
-    A, B = pl.ds(0, half), pl.ds(half, half)
-    F = pl.ds(0, 2 * half)
-    p.greet(p.line_peers())
-    own = pltpu.make_async_copy(b_ref, o_ref.at[p.index()], local_sem)
-    own.start()
-    s, r = Pool(send), Pool(recv)
-    sent = []
-    def push(src_at, rows, to, first=False):
-        i = p.index(*src_at)
-        src = b_ref.at[rows] if first else o_ref.at[i, rows]
-        cp = pltpu.make_async_remote_copy(src_ref=src, dst_ref=o_ref.at[i, rows], send_sem=s.take(),
-            recv_sem=r.take(), device_id=p.dev(*to), device_id_type=MESH)
-        cp.start()
-        sent.append(cp)
-        return cp
-    neg = lambda d, n: (n - d) % n
-    first = {}
-    for d in range(1, nz):
-        first[d] = push((0, 0, 0, 0), F, (d, 0, 0, 0), True)
-    second_a, second_b, third, fourth = {}, {}, {}, []
-    def stage_one(k):
-        if k:
-            first[k].wait_recv()
-        at = (neg(k, nz), 0, 0, 0)
-        for d in range(1, nx):
-            second_a[k, d] = push(at, A, (0, d, 0, 0), k == 0)
-        for d in range(1, ny):
-            second_b[k, d] = push(at, B, (0, 0, d, 0), k == 0)
-        for d in range(1, ny):
-            third["a", k, 0, d] = push(at, A, (0, 0, d, 0), k == 0)
-        for d in range(1, nx):
-            third["b", k, 0, d] = push(at, B, (0, d, 0, 0), k == 0)
-        fourth.append(push(at, F, (0, 0, 0, 1), k == 0))
-    def stage_two(k):
-        for dx in range(1, nx):
-            second_a[k, dx].wait_recv()
-            at = (neg(k, nz), neg(dx, nx), 0, 0)
-            for d in range(1, ny):
-                third["a", k, dx, d] = push(at, A, (0, 0, d, 0))
-            fourth.append(push(at, A, (0, 0, 0, 1)))
-        for dy in range(1, ny):
-            second_b[k, dy].wait_recv()
-            at = (neg(k, nz), 0, neg(dy, ny), 0)
-            for d in range(1, nx):
-                third["b", k, dy, d] = push(at, B, (0, d, 0, 0))
-            fourth.append(push(at, B, (0, 0, 0, 1)))
-    def stage_three(k):
-        for dx in range(nx):
-            for d in range(1, ny):
-                third["a", k, dx, d].wait_recv()
-                fourth.append(push((neg(k, nz), neg(dx, nx), neg(d, ny), 0), A, (0, 0, 0, 1)))
-        for dy in range(ny):
-            for d in range(1, nx):
-                third["b", k, dy, d].wait_recv()
-                fourth.append(push((neg(k, nz), neg(d, nx), neg(dy, ny), 0), B, (0, 0, 0, 1)))
-    for k in range(nz + 2):
-        if k < nz:
-            stage_one(k)
-        if 0 <= k - 1 < nz:
-            stage_two(k - 1)
-        if 0 <= k - 2 < nz:
-            stage_three(k - 2)
-    for cp in fourth:
-        cp.wait_recv()
-    for cp in sent:
-        cp.wait_send()
-    own.wait()
-
-def gather_all(block, cid):
-    nz, nx, ny = grid_of()
-    return pl.pallas_call(gather_all_kernel,
-        out_shape=jax.ShapeDtypeStruct((nz * nx * ny * 2,) + block.shape, block.dtype),
-        in_specs=[VM], out_specs=ANY,
-        scratch_shapes=[pltpu.SemaphoreType.DMA, pltpu.SemaphoreType.DMA((n_sems(nz, nx, ny),)), pltpu.SemaphoreType.DMA((n_sems(nz, nx, ny),))],
-        compiler_params=pltpu.CompilerParams(collective_id=cid, has_side_effects=True),
-        name="gather_all")(block)
-
-def n_sems(nz, nx, ny):
-    return (nz - 1) + nz * (nx - 1 + ny - 1 + 1) + nz * (nx * (ny - 1) + ny * (nx - 1)) + nz * (nx - 1 + ny - 1) + nz * (nx * (ny - 1) + ny * (nx - 1))
-
-def reduce_all_kernel(g_ref, out_ref, acc, rc, ra1, rb1, ra2, rb2, rz, load_sem, send, recv):
-    p = Place()
-    nz, nx, ny = p.nz, p.nx, p.ny
-    rows = g_ref.shape[1]
+    rows = selt_ref.shape[1]
     half = rows // 2
+    f32 = jnp.float32
     A, B = pl.ds(0, half), pl.ds(half, half)
     p.greet(p.line_peers())
     s, r = Pool(send), Pool(recv)
     sent = []
-    order = [(dz, dx, dy) for dx in reversed(range(nx)) for dy in reversed(range(ny)) for dz in range(nz)]
     slot = lambda dz, dx, dy: (dz * nx + dx) * ny + dy
-    neg = lambda d, n: (n - d) % n
+
     def push(src, dst, to):
         cp = pltpu.make_async_remote_copy(src_ref=src, dst_ref=dst, send_sem=s.take(), recv_sem=r.take(),
             device_id=p.dev(*to), device_id_type=MESH)
         cp.start()
         sent.append(cp)
         return cp
-    loads, cores = {}, {}
+
     zs = list(range(1, nz)) + [0]
     plane = [(dx, dy) for dx in reversed(range(nx)) for dy in reversed(range(ny))]
-    for dz in zs:
+    cores, ca, cb, za, zb, zz = {}, {}, {}, {}, {}, {}
+
+    def term(i):
+        return jnp.dot(selt_ref[i], g_ref[i], preferred_element_type=f32)
+
+    def stage_zero(dz):
         for dx, dy in plane:
             k = (dz, dx, dy)
             i = slot(*k)
-            cores[k] = push(g_ref.at[p.index(*k, 1)], rc.at[i], (0, 0, 0, 1))
-            loads[k] = pltpu.make_async_copy(g_ref.at[p.index(*k)], acc.at[i], load_sem.at[i])
-            loads[k].start()
+            give[i] = term(p.index(*k, 1)).astype(give.dtype)
+            cores[k] = push(give.at[i], rc.at[i], (0, 0, 0, 1))
+
     def add(dst, rows_, src):
-        dst_v = acc[dst, rows_, :].astype(jnp.float32) + src[...].astype(jnp.float32)
-        acc[dst, rows_, :] = dst_v.astype(acc.dtype)
-    ca, cb, za, zb, zz = {}, {}, {}, {}, {}
+        acc[dst, rows_, :] = (acc[dst, rows_, :].astype(f32) + src[...].astype(f32)).astype(acc.dtype)
+
     def stage_one(dz):
         for dx, dy in plane:
             k = (dz, dx, dy)
             i = slot(*k)
-            loads[k].wait()
+            mine = term(p.index(*k))
             cores[k].wait_recv()
-            acc[i] = (acc[i].astype(jnp.float32) + rc[i].astype(jnp.float32)).astype(acc.dtype)
+            acc[i] = (mine + rc[i].astype(f32)).astype(acc.dtype)
             if dy:
                 ca[k] = push(acc.at[i, A], ra1.at[dy - 1, dz * nx + dx], (0, 0, dy, 0))
             if dx:
                 cb[k] = push(acc.at[i, B], rb1.at[dx - 1, dz * ny + dy], (0, dx, 0, 0))
+
     def stage_two(dz):
         for dx in reversed(range(nx)):
             for dy in range(1, ny):
@@ -188,6 +113,7 @@
                 add(slot(dz, 0, dy), B, rb1.at[dx - 1, dz * ny + dy])
             if dy:
                 zb[dz, dy] = push(acc.at[slot(dz, 0, dy), B], rb2.at[dy - 1, dz], (0, 0, dy, 0))
+
     def stage_three(dz):
         for dx in range(1, nx):
             za[dz, dx].wait_recv()
@@ -197,45 +123,552 @@
             add(slot(dz, 0, 0), B, rb2.at[dy - 1, dz])
         if dz:
             zz[dz] = push(acc.at[slot(dz, 0, 0)], rz.at[dz - 1], (dz, 0, 0, 0))
+
+    stage_zero(zs[0])
     for k in range(nz + 2):
+        if k + 1 < nz:
+            stage_zero(zs[k + 1])
         if k < nz:
             stage_one(zs[k])
         if 0 <= k - 1 < nz:
             stage_two(zs[k - 1])
         if 0 <= k - 2 < nz:
             stage_three(zs[k - 2])
-    total = acc[slot(0, 0, 0)].astype(jnp.float32)
+    total = acc[slot(0, 0, 0)].astype(f32)
     for dz in range(1, nz):
         zz[dz].wait_recv()
-        total = total + rz[dz - 1].astype(jnp.float32)
-    out_ref[...] = total.astype(out_ref.dtype)
+        total = total + rz[dz - 1].astype(f32)
+    out_ref[...] = total
     for cp in sent:
         cp.wait_send()
 
-def reduce_all(terms, dtype, cid):
+
+def reduce_rows(made, select, cid):
     nz, nx, ny = grid_of()
-    nd, rows, width = terms.shape
-    dt = terms.dtype
+    nd, cap, width = made.shape
+    rows = select.shape[2]
+    dt = made.dtype
     half = rows // 2
-    n = nz * nx * ny + 2 * nz * nx * ny + nz * (nx + ny) + nz
-    blocks = 2 * nz * nx * ny + nz + (nz * (nx + 1) * (ny - 1) + nz * (ny + 1) * (nx - 1)) // 2 + 4
+    n = 3 * nz * nx * ny + nz * (nx + ny) + nz
+    blocks = 3 * nz * nx * ny + nz + (nz * (nx + 1) * (ny - 1) + nz * (ny + 1) * (nx - 1)) // 2 + 4
     parts = 1
-    while blocks * rows * width * 2 // parts > 54 << 20:
+    while (blocks * rows + nd * cap) * width * 2 // parts > 50 << 20:
         parts *= 2
     cols = width // parts
-    one = pl.pallas_call(reduce_all_kernel,
-        out_shape=jax.ShapeDtypeStruct((rows, cols), dtype),
-        in_specs=[ANY], out_specs=VM,
+    one = pl.pallas_call(reduce_rows_kernel,
+        out_shape=jax.ShapeDtypeStruct((rows, cols), jnp.float32),
+        in_specs=[VM, VM], out_specs=VM,
         scratch_shapes=[pltpu.VMEM((nz * nx * ny, rows, cols), dt), pltpu.VMEM((nz * nx * ny, rows, cols), dt),
+            pltpu.VMEM((nz * nx * ny, rows, cols), dt),
             pltpu.VMEM((ny - 1, nz * nx, half, cols), dt), pltpu.VMEM((nx - 1, nz * ny, half, cols), dt),
             pltpu.VMEM((nx - 1, nz, half, cols), dt), pltpu.VMEM((ny - 1, nz, half, cols), dt),
             pltpu.VMEM((nz - 1, rows, cols), dt),
-            pltpu.SemaphoreType.DMA((nz * nx * ny,)), pltpu.SemaphoreType.DMA((n,)), pltpu.SemaphoreType.DMA((n,))],
-        compiler_params=pltpu.CompilerParams(collective_id=cid, has_side_effects=True, vmem_limit_bytes=60 << 20),
-        name="reduce_all")
+            pltpu.SemaphoreType.DMA((n,)), pltpu.SemaphoreType.DMA((n,))],
+        compiler_params=pltpu.CompilerParams(collective_id=cid, has_side_effects=True, vmem_limit_bytes=61 << 20),
+        name="reduce_rows")
+    turned = select.transpose(0, 2, 1)
     if parts == 1:
-        return one(terms)
-    return jnp.concatenate([one(terms[:, :, k * cols:(k + 1) * cols]) for k in range(parts)], axis=1)
+        return one(made, turned)
+    return jnp.concatenate([one(made[:, :, k * cols:(k + 1) * cols], turned) for k in range(parts)], axis=1)
+
+
+def expert_kernel(b_ref, sel_ref, selt_ref, gate_ref, g_ref, win_ref, wout_ref,
+                  all_ref, in_ref, gr_ref, hid_ref, pg_ref, out_ref, back_ref,
+                  xt, gt, in_t, gr_t, hid_t, pg_t, out_t, back_t, local_sem, x_sem, g_sem, store_sem, send, recv):
+    p = Place()
+    nz, nx, ny = p.nz, p.nx, p.ny
+    ns = 2 * ny
+    half = b_ref.shape[0] // 2
+    cap = sel_ref.shape[1]
+    size, width = wout_ref.shape
+    f32, bf = jnp.float32, jnp.bfloat16
+    A, B = pl.ds(0, half), pl.ds(half, half)
+    F = pl.ds(0, 2 * half)
+    p.greet(p.line_peers())
+    own = pltpu.make_async_copy(b_ref, all_ref.at[p.index()], local_sem)
+    own.start()
+    s, r = Pool(send), Pool(recv)
+    sent = []
+    neg = lambda d, n: (n - d) % n
+
+    def push(src_at, rows, to, first=False):
+        i = p.index(*src_at)
+        src = b_ref.at[rows] if first else all_ref.at[i, rows]
+        cp = pltpu.make_async_remote_copy(src_ref=src, dst_ref=all_ref.at[i, rows], send_sem=s.take(),
+            recv_sem=r.take(), device_id=p.dev(*to), device_id_type=MESH)
+        cp.start()
+        sent.append(cp)
+        return cp
+
+    first = {d: push((0, 0, 0, 0), F, (d, 0, 0, 0), True) for d in range(1, nz)}
+    second_a, second_b, third, other = {}, {}, {}, {}
+
+    def cross(at, rows, is_first=False):
+        dx = neg(at[1], nx)
+        other.setdefault((neg(at[0], nz), dx), []).append(push(at, rows, (0, 0, 0, 1), is_first))
+
+    def stage_one(k):
+        if k:
+            first[k].wait_recv()
+        at = (neg(k, nz), 0, 0, 0)
+        for d in range(1, nx):
+            second_a[k, d] = push(at, A, (0, d, 0, 0), k == 0)
+        for d in range(1, ny):
+            second_b[k, d] = push(at, B, (0, 0, d, 0), k == 0)
+        for d in range(1, ny):
+            third["a", k, 0, d] = push(at, A, (0, 0, d, 0), k == 0)
+        for d in range(1, nx):
+            third["b", k, 0, d] = push(at, B, (0, d, 0, 0), k == 0)
+        cross(at, F, k == 0)
+
+    def stage_two(k):
+        for dx in range(1, nx):
+            second_a[k, dx].wait_recv()
+            at = (neg(k, nz), neg(dx, nx), 0, 0)
+            for d in range(1, ny):
+                third["a", k, dx, d] = push(at, A, (0, 0, d, 0))
+            cross(at, A)
+        for dy in range(1, ny):
+            second_b[k, dy].wait_recv()
+            at = (neg(k, nz), 0, neg(dy, ny), 0)
+            for d in range(1, nx):
+                third["b", k, dy, d] = push(at, B, (0, d, 0, 0))
+            cross(at, B)
+
+    def stage_three(k):
+        for dx in range(nx):
+            for d in range(1, ny):
+                third["a", k, dx, d].wait_recv()
+                cross((neg(k, nz), neg(dx, nx), neg(d, ny), 0), A)
+        for dy in range(ny):
+            for d in range(1, nx):
+                third["b", k, dy, d].wait_recv()
+                cross((neg(k, nz), neg(d, nx), neg(dy, ny), 0), B)
+
+    whole = nx * ns <= 8
+    groups = [(k, None) for k in range(nz)] if whole else [(k, dx) for k in range(nz) for dx in range(nx)]
+    gb = nx * ns if whole else ns
+
+    def base_of(i):
+        k, dx = groups[i]
+        z, x, _, _ = p.at(neg(k, nz), neg(dx or 0, nx), 0, 0)
+        return z * nx * ns if whole else (z * nx + x) * ns
+
+    def load_x(i):
+        return pltpu.make_async_copy(all_ref.at[pl.ds(base_of(i), gb)], xt, x_sem)
+
+    def load_g(i):
+        return pltpu.make_async_copy(g_ref.at[pl.ds(base_of(i), gb)], gt.at[i % 2], g_sem.at[i % 2])
+
+    def stores(i, part):
+        rows = pl.ds(base_of(i) * cap, gb * cap)
+        pairs = [[(in_t, in_ref.at[rows]), (gr_t, gr_ref.at[rows])], [(hid_t, hid_ref.at[rows]), (pg_t, pg_ref.at[rows])],
+            [(out_t, out_ref.at[pl.ds(base_of(i), gb)]), (back_t, back_ref.at[rows])]][part]
+        return [pltpu.make_async_copy(a, b, store_sem.at[part, j]) for j, (a, b) in enumerate(pairs)]
+
+    def compute(i):
+        load_x(i).start()
+        if i + 1 < len(groups):
+            load_g(i + 1).start()
+        load_g(i).wait()
+        base = base_of(i)
+        if i:
+            for cp in stores(i - 1, 0):
+                cp.wait()
+        load_x(i).wait()
+
+        def pick(b, carry):
+            rows = pl.ds(pl.multiple_of(b * cap, cap), cap)
+            sel = sel_ref[base + b]
+            in_t[rows, :] = jnp.dot(sel, xt[b], preferred_element_type=f32).astype(bf)
+            gr_t[rows, :] = (jnp.dot(sel, gt[i % 2, b], preferred_element_type=f32) * gate_ref[base + b][:, :1]).astype(bf)
+            return carry
+
+        lax.fori_loop(0, gb, pick, 0)
+        for cp in stores(i, 0):
+            cp.start()
+        if i:
+            for cp in stores(i - 1, 1):
+                cp.wait()
+        wide = min(size, 256)
+
+        def middle(j, carry):
+            left = pl.ds(pl.multiple_of(j * wide, wide), wide)
+            right = pl.ds(pl.multiple_of(size + j * wide, wide), wide)
+            rows_in, rows_grad = in_t[...], gr_t[...]
+            a = jnp.dot(rows_in, win_ref[:, left], preferred_element_type=f32)
+            b = jnp.dot(rows_in, win_ref[:, right], preferred_element_type=f32)
+            h = lax.dot_general(rows_grad, wout_ref[left, :], (((1,), (1,)), ((), ())), preferred_element_type=f32)
+            sigma = 1.0 / (1.0 + jnp.exp(-a))
+            active = a * sigma
+            hid_t[:, left] = (active * b).astype(bf)
+            pg_t[:, left] = (h * b * (sigma * (1.0 + a * (1.0 - sigma)))).astype(bf)
+            pg_t[:, right] = (h * active).astype(bf)
+            return carry
+
+        lax.fori_loop(0, size // wide, middle, 0)
+        for cp in stores(i, 1):
+            cp.start()
+        if i:
+            for cp in stores(i - 1, 2):
+                cp.wait()
+        gates = jnp.concatenate([gate_ref[base + b][:, :1] for b in range(gb)], axis=0)
+
+        def final(j, carry):
+            cols = pl.ds(pl.multiple_of(j * 256, 256), 256)
+            out = jnp.dot(hid_t[...], wout_ref[:, cols], preferred_element_type=f32).astype(bf)
+            weighted = (out.astype(f32) * gates).astype(bf)
+            back_t[:, cols] = lax.dot_general(pg_t[...], win_ref[cols, :], (((1,), (1,)), ((), ())),
+                preferred_element_type=f32).astype(bf)
+            for b in range(gb):
+                out_t[b, :, cols] = jnp.dot(selt_ref[base + b], weighted[b * cap:(b + 1) * cap],
+                    preferred_element_type=f32).astype(bf)
+            return carry
+
+        lax.fori_loop(0, width // 256, final, 0)
+        for cp in stores(i, 2):
+            cp.start()
+
+    load_g(0).start()
+    for k in range(nz + 2):
+        if k < nz:
+            stage_one(k)
+        if 0 <= k - 1 < nz:
+            stage_two(k - 1)
+        if 0 <= k - 2 < nz:
+            stage_three(k - 2)
+            if k == 2:
+                own.wait()
+            for i, (z_group, dx) in enumerate(groups):
+                if z_group == k - 2:
+                    for each in (range(nx) if whole else [dx]):
+                        for cp in other[k - 2, each]:
+                            cp.wait_recv()
+                    compute(i)
+    for part in range(3):
+        for cp in stores(len(groups) - 1, part):
+            cp.wait()
+    for cp in sent:
+        cp.wait_send()
+
+
+def expert_pass(block, select, gate, grads_all, w_in, w_out, cid):
+    nz, nx, ny = grid_of()
+    nd, ns = nz * nx * ny * 2, ny * 2
+    rows, width = block.shape
+    cap, size = select.shape[1], w_out.shape[0]
+    bf = jnp.bfloat16
+    n = n_sems(nz, nx, ny)
+    made = nd * cap
+    gb = nx * ns if nx * ns <= 8 else ns
+    tile = gb * cap
+    sds = jax.ShapeDtypeStruct
+    results = pl.pallas_call(expert_kernel,
+        out_shape=(sds((nd, rows, width), bf), sds((made, width), bf), sds((made, width), bf), sds((made, size), bf),
+            sds((made, 2 * size), bf), sds((nd, rows, width), bf), sds((made, width), bf)),
+        in_specs=[VM, VM, VM, VM, ANY, VM, VM], out_specs=(ANY,) * 7,
+        scratch_shapes=[pltpu.VMEM((gb, rows, width), bf), pltpu.VMEM((2, gb, rows, width), bf),
+            pltpu.VMEM((tile, width), bf), pltpu.VMEM((tile, width), bf), pltpu.VMEM((tile, size), bf),
+            pltpu.VMEM((tile, 2 * size), bf), pltpu.VMEM((gb, rows, width), bf), pltpu.VMEM((tile, width), bf),
+            pltpu.SemaphoreType.DMA, pltpu.SemaphoreType.DMA, pltpu.SemaphoreType.DMA((2,)),
+            pltpu.SemaphoreType.DMA((3, 2)), pltpu.SemaphoreType.DMA((n,)), pltpu.SemaphoreType.DMA((n,))],
+        compiler_params=pltpu.CompilerParams(collective_id=cid, has_side_effects=True, vmem_limit_bytes=61 << 20),
+        name="expert_pass")(block, select, select.transpose(0, 2, 1), jnp.broadcast_to(gate[:, :, None], gate.shape + (128,)),
+            grads_all, w_in, w_out)
+    return results[1:]
+
+
+def expert_reduce_kernel(b_ref, sel_ref, selt_ref, gate_ref, g_ref, win_ref, wout_ref,
+                         all_ref, in_ref, gr_ref, hid_ref, pg_ref, out_ref, sum_ref,
+                         xt, gt, in_t, gr_t, hid_t, pg_t, out_t, back_t, give, acc, rc, ra1, rb1, ra2, rb2, rz,
+                         local_sem, x_sem, g_sem, store_sem, out_sem, send, recv):
+    p = Place()
+    nz, nx, ny = p.nz, p.nx, p.ny
+    ns = 2 * ny
+    half = b_ref.shape[0] // 2
+    cap = sel_ref.shape[1]
+    size, width = wout_ref.shape
+    f32, bf = jnp.float32, jnp.bfloat16
+    A, B = pl.ds(0, half), pl.ds(half, half)
+    F = pl.ds(0, 2 * half)
+    p.greet(p.line_peers())
+    own = pltpu.make_async_copy(b_ref, all_ref.at[p.index()], local_sem)
+    own.start()
+    s, r = Pool(send), Pool(recv)
+    sent = []
+    neg = lambda d, n: (n - d) % n
+
+    def push(src_at, rows, to, first=False):
+        i = p.index(*src_at)
+        src = b_ref.at[rows] if first else all_ref.at[i, rows]
+        cp = pltpu.make_async_remote_copy(src_ref=src, dst_ref=all_ref.at[i, rows], send_sem=s.take(),
+            recv_sem=r.take(), device_id=p.dev(*to), device_id_type=MESH)
+        cp.start()
+        sent.append(cp)
+        return cp
+
+    first = {d: push((0, 0, 0, 0), F, (d, 0, 0, 0), True) for d in range(1, nz)}
+    second_a, second_b, third, other = {}, {}, {}, {}
+
+    def cross(at, rows, is_first=False):
+        dx = neg(at[1], nx)
+        other.setdefault((neg(at[0], nz), dx), []).append(push(at, rows, (0, 0, 0, 1), is_first))
+
+    def stage_one(k):
+        if k:
+            first[k].wait_recv()
+        at = (neg(k, nz), 0, 0, 0)
+        for d in range(1, nx):
+            second_a[k, d] = push(at, A, (0, d, 0, 0), k == 0)
+        for d in range(1, ny):
+            second_b[k, d] = push(at, B, (0, 0, d, 0), k == 0)
+        for d in range(1, ny):
+            third["a", k, 0, d] = push(at, A, (0, 0, d, 0), k == 0)
+        for d in range(1, nx):
+            third["b", k, 0, d] = push(at, B, (0, d, 0, 0), k == 0)
+        cross(at, F, k == 0)
+
+    def stage_two(k):
+        for dx in range(1, nx):
+            second_a[k, dx].wait_recv()
+            at = (neg(k, nz), neg(dx, nx), 0, 0)
+            for d in range(1, ny):
+                third["a", k, dx, d] = push(at, A, (0, 0, d, 0))
+            cross(at, A)
+        for dy in range(1, ny):
+            second_b[k, dy].wait_recv()
+            at = (neg(k, nz), 0, neg(dy, ny), 0)
+            for d in range(1, nx):
+                third["b", k, dy, d] = push(at, B, (0, d, 0, 0))
+            cross(at, B)
+
+    def stage_three(k):
+        for dx in range(nx):
+            for d in range(1, ny):
+                third["a", k, dx, d].wait_recv()
+                cross((neg(k, nz), neg(dx, nx), neg(d, ny), 0), A)
+        for dy in range(ny):
+            for d in range(1, nx):
+                third["b", k, dy, d].wait_recv()
+                cross((neg(k, nz), neg(d, nx), neg(dy, ny), 0), B)
+
+    gb = nx * ns
+
+    def base_of(i):
+        return p.at(neg(i, nz), 0, 0, 0)[0] * gb
+
+    def load_x(i):
+        return pltpu.make_async_copy(all_ref.at[pl.ds(base_of(i), gb)], xt, x_sem)
+
+    def load_g(i):
+        return pltpu.make_async_copy(g_ref.at[pl.ds(base_of(i), gb)], gt, g_sem)
+
+    def stores(i, part):
+        rows = pl.ds(base_of(i) * cap, gb * cap)
+        pairs = [[(in_t, in_ref.at[rows]), (gr_t, gr_ref.at[rows])], [(hid_t, hid_ref.at[rows]), (pg_t, pg_ref.at[rows])]][part]
+        return [pltpu.make_async_copy(a, b, store_sem.at[part, j]) for j, (a, b) in enumerate(pairs)]
+
+    def compute(i):
+        load_x(i).start()
+        load_g(i).wait()
+        base = base_of(i)
+        if i:
+            for cp in stores(i - 1, 0):
+                cp.wait()
+        load_x(i).wait()
+
+        def pick(b, carry):
+            rows = pl.ds(pl.multiple_of(b * cap, cap), cap)
+            sel = sel_ref[base + b]
+            in_t[rows, :] = jnp.dot(sel, xt[b], preferred_element_type=f32).astype(bf)
+            gr_t[rows, :] = (jnp.dot(sel, gt[b], preferred_element_type=f32) * gate_ref[base + b][:, :1]).astype(bf)
+            return carry
+
+        lax.fori_loop(0, gb, pick, 0)
+        if i + 1 < nz:
+            load_g(i + 1).start()
+        for cp in stores(i, 0):
+            cp.start()
+        if i:
+            for cp in stores(i - 1, 1):
+                cp.wait()
+        wide = min(size, 256)
+
+        def middle(j, carry):
+            left = pl.ds(pl.multiple_of(j * wide, wide), wide)
+            right = pl.ds(pl.multiple_of(size + j * wide, wide), wide)
+            rows_in, rows_grad = in_t[...], gr_t[...]
+            a = jnp.dot(rows_in, win_ref[:, left], preferred_element_type=f32)
+            b = jnp.dot(rows_in, win_ref[:, right], preferred_element_type=f32)
+            h = lax.dot_general(rows_grad, wout_ref[left, :], (((1,), (1,)), ((), ())), preferred_element_type=f32)
+            sigma = 1.0 / (1.0 + jnp.exp(-a))
+            active = a * sigma
+            hid_t[:, left] = (active * b).astype(bf)
+            pg_t[:, left] = (h * b * (sigma * (1.0 + a * (1.0 - sigma)))).astype(bf)
+            pg_t[:, right] = (h * active).astype(bf)
+            return carry
+
+        lax.fori_loop(0, size // wide, middle, 0)
+        for cp in stores(i, 1):
+            cp.start()
+        gates = jnp.concatenate([gate_ref[base + b][:, :1] for b in range(gb)], axis=0)
+
+        def out_copy(j):
+            t = lax.rem(j, 2)
+            cols = pl.ds(pl.multiple_of(j * 256, 256), 256)
+            return pltpu.make_async_copy(out_t.at[t], out_ref.at[pl.ds(base, gb), :, cols], out_sem.at[t])
+
+        def final(j, carry):
+            cols = pl.ds(pl.multiple_of(j * 256, 256), 256)
+            out = jnp.dot(hid_t[...], wout_ref[:, cols], preferred_element_type=f32).astype(bf)
+            weighted = (out.astype(f32) * gates).astype(bf)
+            back_t[:, cols] = lax.dot_general(pg_t[...], win_ref[cols, :], (((1,), (1,)), ((), ())),
+                preferred_element_type=f32).astype(bf)
+
+            @pl.when(j >= 2)
+            def _():
+                out_copy(j - 2).wait()
+
+            for b in range(gb):
+                out_t[lax.rem(j, 2), b] = jnp.dot(selt_ref[base + b], weighted[b * cap:(b + 1) * cap],
+                    preferred_element_type=f32).astype(bf)
+            out_copy(j).start()
+            return carry
+
+        steps = width // 256
+        lax.fori_loop(0, steps, final, 0)
+        for j in range(max(0, steps - 2), steps):
+            out_copy(j).wait()
+
+    plane = [(dx, dy) for dx in reversed(range(nx)) for dy in reversed(range(ny))]
+    slot = lambda dz, dx, dy: (dz * nx + dx) * ny + dy
+    cores, ca, cb, za, zb, zz = {}, {}, {}, {}, {}, {}
+    done = []
+
+    def push_to(src, dst, to):
+        cp = pltpu.make_async_remote_copy(src_ref=src, dst_ref=dst, send_sem=s.take(), recv_sem=r.take(),
+            device_id=p.dev(*to), device_id_type=MESH)
+        cp.start()
+        sent.append(cp)
+        return cp
+
+    def term(i, index):
+        b = index - base_of(i)
+        rows = pl.ds(pl.multiple_of(b * cap, cap), cap)
+        return jnp.dot(selt_ref[index], back_t[rows, :], preferred_element_type=f32)
+
+    def add(dst, rows_, src):
+        acc[dst, rows_, :] = (acc[dst, rows_, :].astype(f32) + src[...].astype(f32)).astype(acc.dtype)
+
+    def sum_one(i):
+        dz = neg(i, nz)
+        for j, (dx, dy) in enumerate(plane):
+            g = (i % 2) * len(plane) + j
+            if i >= 2:
+                old = cores[neg(i - 2, nz), dx, dy]
+                old.wait_send()
+                done.append(old)
+            give[g] = term(i, p.index(dz, dx, dy, 1)).astype(bf)
+            cores[dz, dx, dy] = push_to(give.at[g], rc.at[slot(dz, dx, dy)], (0, 0, 0, 1))
+        for dx, dy in plane:
+            t = slot(dz, dx, dy)
+            mine = term(i, p.index(dz, dx, dy))
+            cores[dz, dx, dy].wait_recv()
+            acc[t] = (mine + rc[t].astype(f32)).astype(bf)
+            if dy:
+                ca[dz, dx, dy] = push_to(acc.at[t, A], ra1.at[dy - 1, dz * nx + dx], (0, 0, dy, 0))
+            if dx:
+                cb[dz, dx, dy] = push_to(acc.at[t, B], rb1.at[dx - 1, dz * ny + dy], (0, dx, 0, 0))
+
+    def sum_two(i):
+        dz = neg(i, nz)
+        for dx in reversed(range(nx)):
+            for dy in range(1, ny):
+                ca[dz, dx, dy].wait_recv()
+                add(slot(dz, dx, 0), A, ra1.at[dy - 1, dz * nx + dx])
+            if dx:
+                za[dz, dx] = push_to(acc.at[slot(dz, dx, 0), A], ra2.at[dx - 1, dz], (0, dx, 0, 0))
+        for dy in reversed(range(ny)):
+            for dx in range(1, nx):
+                cb[dz, dx, dy].wait_recv()
+                add(slot(dz, 0, dy), B, rb1.at[dx - 1, dz * ny + dy])
+            if dy:
+                zb[dz, dy] = push_to(acc.at[slot(dz, 0, dy), B], rb2.at[dy - 1, dz], (0, 0, dy, 0))
+
+    def sum_three(i):
+        dz = neg(i, nz)
+        for dx in range(1, nx):
+            za[dz, dx].wait_recv()
+            add(slot(dz, 0, 0), A, ra2.at[dx - 1, dz])
+        for dy in range(1, ny):
+            zb[dz, dy].wait_recv()
+            add(slot(dz, 0, 0), B, rb2.at[dy - 1, dz])
+        if dz:
+            zz[dz] = push_to(acc.at[slot(dz, 0, 0)], rz.at[dz - 1], (dz, 0, 0, 0))
+
+    load_g(0).start()
+    for k in range(nz + 2):
+        if k < nz:
+            stage_one(k)
+        if 0 <= k - 1 < nz:
+            stage_two(k - 1)
+        if 0 <= k - 2 < nz:
+            stage_three(k - 2)
+            if k == 2:
+                own.wait()
+            for dx in range(nx):
+                for cp in other[k - 2, dx]:
+                    cp.wait_recv()
+            compute(k - 2)
+            sum_one(k - 2)
+            if k - 3 >= 0:
+                sum_two(k - 3)
+            if k - 4 >= 0:
+                sum_three(k - 4)
+    sum_two(nz - 1)
+    for i in range(max(0, nz - 2), nz):
+        sum_three(i)
+    total = acc[slot(0, 0, 0)].astype(f32)
+    for dz in range(1, nz):
+        zz[dz].wait_recv()
+        total = total + rz[dz - 1].astype(f32)
+    sum_ref[...] = total
+    for part in range(2):
+        for cp in stores(nz - 1, part):
+            cp.wait()
+    for cp in sent:
+        if not any(cp is other_cp for other_cp in done):
+            cp.wait_send()
+
+
+def expert_reduce(block, select, gate, grads_all, w_in, w_out, cid):
+    nz, nx, ny = grid_of()
+    nd, gb = nz * nx * ny * 2, nx * ny * 2
+    rows, width = block.shape
+    half = rows // 2
+    cap, size = select.shape[1], w_out.shape[0]
+    bf = jnp.bfloat16
+    n = n_sems(nz, nx, ny) + 2 * nz * nx * ny + nz * (nx + ny) + 2 * nz * (nx * (ny - 1) + ny * (nx - 1))
+    made, tile, slots = nd * cap, gb * cap, nz * nx * ny
+    sds = jax.ShapeDtypeStruct
+    results = pl.pallas_call(expert_reduce_kernel,
+        out_shape=(sds((nd, rows, width), bf), sds((made, width), bf), sds((made, width), bf), sds((made, size), bf),
+            sds((made, 2 * size), bf), sds((nd, rows, width), bf), sds((rows, width), jnp.float32)),
+        in_specs=[VM, VM, VM, VM, ANY, VM, VM], out_specs=(ANY,) * 6 + (VM,),
+        scratch_shapes=[pltpu.VMEM((gb, rows, width), bf), pltpu.VMEM((gb, rows, width), bf),
+            pltpu.VMEM((tile, width), bf), pltpu.VMEM((tile, width), bf), pltpu.VMEM((tile, size), bf),
+            pltpu.VMEM((tile, 2 * size), bf), pltpu.VMEM((2, gb, rows, 256), bf), pltpu.VMEM((tile, width), bf),
+            pltpu.VMEM((2 * nx * ny, rows, width), bf), pltpu.VMEM((slots, rows, width), bf), pltpu.VMEM((slots, rows, width), bf),
+            pltpu.VMEM((ny - 1, nz * nx, half, width), bf), pltpu.VMEM((nx - 1, nz * ny, half, width), bf),
+            pltpu.VMEM((nx - 1, nz, half, width), bf), pltpu.VMEM((ny - 1, nz, half, width), bf),
+            pltpu.VMEM((nz - 1, rows, width), bf),
+            pltpu.SemaphoreType.DMA, pltpu.SemaphoreType.DMA, pltpu.SemaphoreType.DMA,
+            pltpu.SemaphoreType.DMA((2, 2)), pltpu.SemaphoreType.DMA((2,)),
+            pltpu.SemaphoreType.DMA((n,)), pltpu.SemaphoreType.DMA((n,))],
+        compiler_params=pltpu.CompilerParams(collective_id=cid, has_side_effects=True, vmem_limit_bytes=67043328),
+        name="expert_reduce")(block, select, select.transpose(0, 2, 1), jnp.broadcast_to(gate[:, :, None], gate.shape + (128,)),
+            grads_all, w_in, w_out)
+    return results[1:]
 
 
 def shard_peers(ny):
@@ -609,19 +1042,122 @@
 THETA = 1000000.0
 
 
-def norm_rows(values_in, gain):
-    return values_in * lax.rsqrt(jnp.mean(values_in * values_in, axis=-1, keepdims=True) + EPSILON) * gain
-
-
-def rotate(vectors, position):
-    half_size = vectors.shape[-1] // 2
-    freqs = jnp.exp(jnp.arange(half_size, dtype=jnp.float32) * (-2.0 * math.log(THETA) / vectors.shape[-1]))
-    angles = position[:, None] * freqs[None, :]
-    cosine = jnp.cos(angles)[:, None, :]
-    sine = jnp.sin(angles)[:, None, :]
-    first = vectors[..., :half_size]
-    second = vectors[..., half_size:]
-    return jnp.concatenate([first * cosine - second * sine, second * cosine + first * sine], axis=-1)
+def normed(raw, gain):
+    scale = lax.rsqrt(jnp.mean(raw * raw, axis=-1, keepdims=True) + EPSILON)
+    hat = raw * scale
+    return scale, hat, hat * gain
+
+
+def turned(v, cosine, sine):
+    return v * cosine + pltpu.roll(v, HEAD // 2, 1) * sine
+
+
+def turned_back(g, cosine, sine):
+    return g * cosine + pltpu.roll(g * sine, HEAD // 2, 1)
+
+
+def weights_of(queries, keys, mask):
+    scores = lax.dot_general(queries, keys, (((1,), (1,)), ((), ())), preferred_element_type=jnp.float32)
+    scores = scores * HEAD ** (-0.5) + mask
+    highest = jnp.max(scores, axis=-1, keepdims=True)
+    powers = jnp.exp(scores - highest)
+    return powers * (1.0 / jnp.sum(powers, axis=-1, keepdims=True))
+
+
+def attend_kernel(q_ref, k_ref, v_ref, gq_ref, gk_ref, cos_ref, sin_ref, mask_ref, o_ref):
+    bf = jnp.bfloat16
+    cosine, sine = cos_ref[...], sin_ref[...]
+    queries = turned(normed(q_ref[...], gq_ref[...])[2], cosine, sine).astype(bf)
+    keys = turned(normed(k_ref[...], gk_ref[...])[2], cosine, sine).astype(bf)
+    probs = weights_of(queries, keys, mask_ref[...]).astype(bf)
+    o_ref[...] = jnp.dot(probs, v_ref[...].astype(bf), preferred_element_type=jnp.float32).astype(bf)
+
+
+def attend_back_kernel(per, q_ref, k_ref, v_ref, gq_ref, gk_ref, cos_ref, sin_ref, mask_ref, o_ref, do_ref, inv_ref,
+                       dq_ref, dk_ref, dv_ref, dgq_ref, dgk_ref, dk_acc, dv_acc):
+    bf, f32 = jnp.bfloat16, jnp.float32
+    h = pl.program_id(0)
+    cosine, sine = cos_ref[...], sin_ref[...]
+    gain_q, gain_k = gq_ref[...], gk_ref[...]
+    q_scale, q_hat, q_gained = normed(q_ref[...], gain_q)
+    k_scale, k_hat, k_gained = normed(k_ref[...], gain_k)
+    queries = turned(q_gained, cosine, sine).astype(bf)
+    keys = turned(k_gained, cosine, sine).astype(bf)
+    probs = weights_of(queries, keys, mask_ref[...])
+    out_grad = do_ref[...]
+    delta = jnp.sum(out_grad.astype(f32) * o_ref[...].astype(f32), axis=-1, keepdims=True)
+    prob_grad = lax.dot_general(out_grad, v_ref[...].astype(bf), (((1,), (1,)), ((), ())), preferred_element_type=f32)
+    score_grad = (probs * (prob_grad - delta)).astype(bf)
+    factor = HEAD ** (-0.5)
+    over_rows = (((0,), (0,)), ((), ()))
+    dk_here = lax.dot_general(score_grad, queries, over_rows, preferred_element_type=f32)
+    dv_here = lax.dot_general(probs.astype(bf), out_grad, over_rows, preferred_element_type=f32)
+
+    @pl.when(h % per == 0)
+    def _():
+        dk_acc[...] = dk_here
+        dv_acc[...] = dv_here
+
+    @pl.when(h % per != 0)
+    def _():
+        dk_acc[...] += dk_here
+        dv_acc[...] += dv_here
+
+    @pl.when(h == 0)
+    def _():
+        dgq_ref[...] = jnp.zeros_like(dgq_ref)
+        dgk_ref[...] = jnp.zeros_like(dgk_ref)
+
+    def raw_grad(grad, scale, hat, gain, gain_grad_ref):
+        gained = turned_back(grad, cosine, sine)
+        gain_grad_ref[0:1, :] += jnp.sum(gained * hat, axis=0, keepdims=True)
+        inner = gained * gain
+        return scale * (inner - hat * jnp.mean(inner * hat, axis=-1, keepdims=True))
+
+    query_grad = jnp.dot(score_grad, keys, preferred_element_type=f32) * factor
+    dq_ref[...] = (raw_grad(query_grad, q_scale, q_hat, gain_q, dgq_ref) * inv_ref[...]).astype(bf)
+
+    @pl.when(h % per == per - 1)
+    def _():
+        dk_ref[...] = (raw_grad(dk_acc[...] * factor, k_scale, k_hat, gain_k, dgk_ref) * inv_ref[...]).astype(bf)
+        dv_ref[...] = (dv_acc[...] * inv_ref[...]).astype(bf)
+
+
+def head_specs(length, heads, kv_heads, per):
+    block = (length, HEAD)
+    same = lambda h: (0, 0)
+    return block, [pl.BlockSpec(block, lambda h: (0, h)), pl.BlockSpec(block, lambda h: (0, heads + h // per)),
+        pl.BlockSpec(block, lambda h: (0, heads + kv_heads + h // per)), pl.BlockSpec((1, HEAD), same),
+        pl.BlockSpec((1, HEAD), same), pl.BlockSpec(block, same), pl.BlockSpec(block, same),
+        pl.BlockSpec((length, length), same)]
+
+
+def attend(projected, shared, heads, kv_heads):
+    length = projected.shape[0]
+    block, specs = head_specs(length, heads, kv_heads, heads // kv_heads)
+    return pl.pallas_call(attend_kernel, grid=(heads,),
+        out_shape=jax.ShapeDtypeStruct((length, heads * HEAD), jnp.bfloat16),
+        in_specs=specs, out_specs=pl.BlockSpec(block, lambda h: (0, h)),
+        compiler_params=pltpu.CompilerParams(vmem_limit_bytes=56 << 20),
+        name="attend")(projected, projected, projected, *shared)
+
+
+def attend_back(projected, shared, attn, attn_grad, inverse, heads, kv_heads):
+    length = projected.shape[0]
+    per = heads // kv_heads
+    block, specs = head_specs(length, heads, kv_heads, per)
+    at_head = pl.BlockSpec(block, lambda h: (0, h))
+    at_group = pl.BlockSpec(block, lambda h: (0, h // per))
+    small = pl.BlockSpec((8, HEAD), lambda h: (0, 0))
+    sds, bf, f32 = jax.ShapeDtypeStruct, jnp.bfloat16, jnp.float32
+    return pl.pallas_call(functools.partial(attend_back_kernel, per), grid=(heads,),
+        out_shape=(sds((length, heads * HEAD), bf), sds((length, kv_heads * HEAD), bf), sds((length, kv_heads * HEAD), bf),
+            sds((8, HEAD), f32), sds((8, HEAD), f32)),
+        in_specs=specs + [at_head, at_head, pl.BlockSpec((length, 1), lambda h: (0, 0))],
+        out_specs=(at_head, at_group, at_group, small, small),
+        scratch_shapes=[pltpu.VMEM(block, f32), pltpu.VMEM(block, f32)],
+        compiler_params=pltpu.CompilerParams(vmem_limit_bytes=58 << 20),
+        name="attend_back")(projected, projected, projected, *shared, attn, attn_grad, inverse)
 
 
 def segment_starts(segment):
@@ -637,12 +1173,9 @@
     nd = n_expert * n_shard
     rows, width = tokens_in.shape
     me = lax.axis_index("expert") * n_shard + lax.axis_index("shard")
-    shard = lax.axis_index("shard")
     heads = QUERY_HEADS // n_shard
-    group = QUERY_HEADS // KEY_VALUE_HEADS
     kv_heads = max(1, KEY_VALUE_HEADS // n_shard)
     copies = max(1, n_shard // KEY_VALUE_HEADS)
-    per = heads // kv_heads
     q_cols, kv_cols = heads * HEAD, kv_heads * HEAD
     q_all, kv_all = QUERY_HEADS * HEAD, KEY_VALUE_HEADS * HEAD
     wide = qkv_weight.shape[0]
@@ -674,8 +1207,9 @@
         at += g.shape[0]
     extra = jnp.concatenate([expert_ids.astype(bf), high, middle, low, gains[:, None]], axis=1)
     extra = jnp.pad(extra, ((0, 0), (0, 128 - extra.shape[1])))
-    grads_all = gather_all(jnp.concatenate([out_grad, extra], axis=1), 1)
-    info = grads_all[:, :, width:].astype(f32)
+    both = ("expert", "shard")
+    info = lax.all_gather(extra, both, axis=0, tiled=False).astype(f32)
+    grads_all = lax.all_gather(out_grad, both, axis=0, tiled=True).reshape(nd, rows, width)
     ids_all = info[:, :, :top]
     weights_all = info[:, :, top:2 * top] + info[:, :, 2 * top:3 * top] + info[:, :, 3 * top:4 * top]
     gain_col = info[:, :, 4 * top]
@@ -690,33 +1224,19 @@
     segment = segment_ids[0]
     index = jnp.arange(length, dtype=jnp.int32)
     position = (index - segment_starts(segment)).astype(f32)
-    query_raw = projected[:, :q_cols].reshape(length, heads, HEAD)
-    key_raw = projected[:, q_cols:q_cols + kv_cols].reshape(length, kv_heads, HEAD)
-    values = projected[:, q_cols + kv_cols:].astype(bf).reshape(length, kv_heads, HEAD)
-
-    def prepare(query_in, key_in, gain_q, gain_k):
-        return rotate(norm_rows(query_in, gain_q), position), rotate(norm_rows(key_in, gain_k), position)
-
-    (query_rot, key_rot), prepare_back = jax.vjp(prepare, query_raw, key_raw, query_gain, key_gain)
-    queries = query_rot.astype(bf).reshape(length, kv_heads, per, HEAD)
-    keys = key_rot.astype(bf)
+    freqs = jnp.exp(jnp.arange(HEAD // 2, dtype=f32) * (-2.0 * math.log(THETA) / HEAD))
+    angles = position[:, None] * freqs[None, :]
+    cosine, sine = jnp.cos(angles), jnp.sin(angles)
     allowed = (segment[:, None] == segment[None, :]) & (index[None, :] <= index[:, None])
-    factor = HEAD ** (-0.5)
-    scores = jnp.einsum("tkgd,skd->kgts", queries, keys, preferred_element_type=f32) * factor
-    scores = jnp.where(allowed[None, None], scores, -1e30)
-    highest = jnp.max(scores, axis=-1, keepdims=True)
-    log_total = highest + jnp.log(jnp.sum(jnp.exp(scores - highest), axis=-1, keepdims=True))
-    probs = jnp.exp(scores - log_total)
-    probs_low = probs.astype(bf)
-    attn = jnp.einsum("kgts,skd->tkgd", probs_low, values, preferred_element_type=f32).astype(bf)
-    attn_flat = attn.reshape(length, q_cols)
+    shared = (query_gain[None], key_gain[None], jnp.concatenate([cosine, cosine], axis=1),
+        jnp.concatenate([-sine, sine], axis=1), jnp.where(allowed, 0.0, -1e30).astype(f32))
+    attn_flat = attend(projected, shared, heads, kv_heads)
     mixed = jnp.dot(attn_flat, out_rows, preferred_element_type=f32).astype(bf)
     hidden_state = tokens_in.astype(f32) + pack_reduce(mixed.reshape(n_shard, rows, width), 2)
     hidden_inverse = lax.rsqrt(jnp.mean(hidden_state * hidden_state, axis=-1, keepdims=True) + EPSILON)
     hidden_norm = hidden_state * hidden_inverse
     moe_in = (hidden_norm * moe_scale).astype(bf)
 
-    rows_all = gather_all(moe_in, 3)
     cap = max(2, 2 * rows * top // nd)
     hit = ids_all == me.astype(f32)
     any_hit = jnp.any(hit, axis=-1)
@@ -726,48 +1246,29 @@
     chosen = (jnp.arange(cap, dtype=f32)[None, :, None] == rank[:, None, :]) & any_hit[:, None, :]
     slot_gate = jnp.sum(jnp.where(chosen, gate[:, None, :], 0.0), axis=-1)
     select = chosen.astype(bf)
-    in_rows = jnp.einsum("bkt,btd->bkd", select, rows_all, preferred_element_type=f32).astype(bf).reshape(nd * cap, width)
-    grad_rows = (jnp.einsum("bkt,btd->bkd", select, grads_all[:, :, :width], preferred_element_type=f32)
-        * slot_gate[:, :, None]).astype(bf).reshape(nd * cap, width)
-    w_in, w_out = expert_in[0], expert_out[0]
-    size = w_out.shape[0]
-    pre = jnp.dot(in_rows, w_in, preferred_element_type=f32)
-    gate_part, up_part = pre[:, :size], pre[:, size:]
-    sigma = jax.nn.sigmoid(gate_part)
-    active = gate_part * sigma
-    hidden = (active * up_part).astype(bf)
-    outputs = jnp.dot(hidden, w_out, preferred_element_type=f32).astype(bf)
-    weighted = (outputs.astype(f32) * slot_gate.reshape(-1, 1)).astype(bf).reshape(nd, cap, width)
-    out_terms = jnp.einsum("bkt,bkd->btd", select, weighted, preferred_element_type=f32).astype(bf)
-    moe_sum = reduce_all(out_terms, f32, 4)
-    hidden_grad = jnp.einsum("rd,fd->rf", grad_rows, w_out, preferred_element_type=f32)
-    gate_grad = hidden_grad * up_part * (sigma * (1.0 + gate_part * (1.0 - sigma)))
-    pre_grad = jnp.concatenate([gate_grad, hidden_grad * active], axis=-1).astype(bf)
-    rows_grad = jnp.einsum("rc,dc->rd", pre_grad, w_in, preferred_element_type=f32).astype(bf).reshape(nd, cap, width)
-    grad_terms = jnp.einsum("bkt,bkd->btd", select, rows_grad, preferred_element_type=f32).astype(bf)
-    moe_grad = reduce_all(grad_terms, f32, 5)
+    experts = (moe_in, select, slot_gate, grads_all, expert_in[0], expert_out[0])
+    if 16 * nd * rows * width // 5 <= 28 << 20:
+        in_rows, grad_rows, hidden, pre_grad, out_terms, moe_grad = expert_reduce(*experts, 3)
+    else:
+        in_rows, grad_rows, hidden, pre_grad, out_terms, rows_grad = expert_pass(*experts, 1)
+        moe_grad = reduce_rows(rows_grad.reshape(nd, cap, width), select, 5)
     expert_in_grad = jnp.einsum("rd,rc->dc", in_rows, pre_grad, preferred_element_type=f32)[None]
     expert_out_grad = jnp.einsum("rf,rd->fd", hidden, grad_rows, preferred_element_type=f32)[None]
-    block_output = (hidden_state + moe_sum).astype(bf)
 
     scaled_grad = moe_grad * moe_scale
     moe_gain_grad = jnp.sum(moe_grad * hidden_norm, axis=0)
     residual = out_grad.astype(f32) + hidden_inverse * (
         scaled_grad - hidden_norm * jnp.mean(scaled_grad * hidden_norm, axis=-1, keepdims=True))
     residual_pack = pack_gather(residual.astype(bf), 6).reshape(length, width)
+    out_terms, residual_pack = lax.optimization_barrier((out_terms, residual_pack))
+    moe_sum = lax.psum_scatter(out_terms.reshape(nd * rows, width), both, scatter_dimension=0, tiled=True).astype(f32)
+    block_output = (hidden_state + moe_sum).astype(bf)
     out_term = jnp.einsum("tc,td->cd", attn_flat, residual_pack, preferred_element_type=f32).astype(bf)
     attn_grad = jnp.einsum("td,cd->tc", residual_pack, out_rows, preferred_element_type=f32).astype(bf)
-    attn_grad = attn_grad.reshape(length, kv_heads, per, HEAD)
-    delta = jnp.einsum("tkgd,tkgd->kgt", attn_grad, attn, preferred_element_type=f32)
-    prob_grad = jnp.einsum("tkgd,skd->kgts", attn_grad, values, preferred_element_type=f32)
-    score_grad = (probs * (prob_grad - delta[..., None])).astype(bf)
-    query_grad = jnp.einsum("kgts,skd->tkgd", score_grad, keys, preferred_element_type=f32) * factor
-    key_grad = jnp.einsum("kgts,tkgd->skd", score_grad, queries, preferred_element_type=f32) * factor
-    value_grad = jnp.einsum("kgts,tkgd->skd", probs_low, attn_grad, preferred_element_type=f32)
-    query_back, key_back, query_gain_grad, key_gain_grad = prepare_back((query_grad.reshape(length, heads, HEAD), key_grad))
-    projected_grad = jnp.concatenate([query_back.reshape(length, -1), key_back.reshape(length, -1),
-        value_grad.reshape(length, -1)], axis=1)
-    projected_grad = (projected_grad * inverse).astype(bf)
+    query_part, key_part, value_part, query_gain_grad, key_gain_grad = attend_back(projected, shared, attn_flat, attn_grad,
+        inverse, heads, kv_heads)
+    query_gain_grad, key_gain_grad = query_gain_grad[0], key_gain_grad[0]
+    projected_grad = jnp.concatenate([query_part, key_part, value_part], axis=1)
     qkv_term = jnp.einsum("td,tc->dc", pack, projected_grad, preferred_element_type=f32).astype(bf)
     input_term = jnp.einsum("tc,dc->td", projected_grad, weights, preferred_element_type=f32).astype(bf)
 
@@ -775,6 +1276,7 @@
         v = v.reshape(nd, -1)
         return jnp.pad(v, ((0, 0), (0, 128 - v.shape[1])))[:, None]
 
+    expert_in_grad, expert_out_grad, input_term = lax.optimization_barrier((expert_in_grad, expert_out_grad, input_term))
     small = jnp.concatenate([lanes(moe_gain_grad), lanes(query_gain_grad), lanes(key_gain_grad),
         jnp.zeros((nd, 5, 128), f32)], axis=1)
     out_weight_grad, qkv_part, small_sum, input_sum = reduce_grads(out_term.reshape(n_expert, -1, width),

time: 1020 us -> 831 us (0.81); the launches traced: 1000 us -> 826 us
  matrix products: 195 us -> 60.8 us
  other arithmetic: 56.3 us -> 29.8 us
  Pallas kernels: 720 us -> 701 us
  local copies, waits for them, and re-layouts: 31 us -> 18.1 us
  between operations: 2.04 us -> 14.5 us
    dot_general x14 -> x0, matrix products: 133 us -> none  [the longest x1 19.2 us: shards(): jnp.einsum('rc,dc->rd', pre_grad, w_in, preferred_element_type=f32)]
    pallas_call x4 -> x3, Pallas kernels: 377 us -> 291 us  [the longest x1 244 us: expert_reduce(): pl.pallas_call(expert_reduce_kernel, out_shape=(sds((nd, rows, width), bf...]
    pallas_call x1, Pallas kernels: 150 us -> 197 us  [reduce_grads(): pl.pallas_call(grads_kernel, out_shape=(jax.ShapeDtypeStruct((rows_o, wid...]
    pallas_call x1, Pallas kernels: 159 us -> 184 us  [gather_weights(): pl.pallas_call(weights_kernel, out_shape=(jax.ShapeDtypeStruct((ne * ns,)...]
    unnamed x146 -> x79, local copies, waits for them, and re-layouts: 18.7 us -> 7.51 us
  transfers between devices with their start and end apart: 0 -> 3, of which waited for: 0 -> 0; matrix products, arithmetic and copies ran while one was open for 0% -> 11% of each run, Pallas kernels for 0% -> 54%
where the time goes in v2:
time: 831 us; the launch traced here: 826 us
  Pallas kernels  701 us (84%)
  matrix products  60.8 us (7%)
  other arithmetic  29.8 us (4%)
  local copies, waits for them, and re-layouts  18.1 us (2%)
  between operations  14.5 us (2%)
    pallas_call x1, Pallas kernels, expert_reduce(): pl.pallas_call(expert_reduce_kernel, out_shape=(sds((nd, rows, width), bf...  244 us
    pallas_call x1, Pallas kernels, reduce_grads(): pl.pallas_call(grads_kernel, out_shape=(jax.ShapeDtypeStruct((rows_o, wid...  197 us
    pallas_call x1, Pallas kernels, gather_weights(): pl.pallas_call(weights_kernel, out_shape=(jax.ShapeDtypeStruct((ne * ns,)...  184 us
    pallas_call x1, Pallas kernels, attend_back(): pl.pallas_call(functools.partial(attend_back_kernel, per), grid=(heads,),...  28.9 us
    pallas_call x1, Pallas kernels, attend(): pl.pallas_call(attend_kernel, grid=(heads,), out_shape=jax.ShapeDtypeStru...  18.2 us
  transfers between devices with their start and end apart: 3, of which 0 were waited for; matrix products, arithmetic and copies ran while one was open for 11% of the time, Pallas kernels for 54%

profile of v2, /device:TPU:2, one launch (start us, length us, event | category | flops | bytes accessed | tf_op | source)
XLA Modules:
  0.0 825.6 jit_solution(2207356366250327635)
XLA Ops:
  7.9 0.7 constant_dynamic-update-slice_fusion.3
  8.6 0.8 constant_dynamic-update-slice_fusion.2
  9.4 0.8 constant_dynamic-update-slice_fusion.1
  10.8 0.8 dynamic_update_slice.12
  11.7 0.9 dynamic_update_slice.13
  13.2 0.7 all-gather.4.cloned.1.call-update
  14.6 1.3 fusion.2
  16.1 0.9 maximum_bitcast_fusion.w_ref
  17.0 183.9 %gather_weights.1 = (bf16[32,64,1280]{2,1,0:T(8,128)(2,1)}, bf16[8,128,2048]{2,1,0:T(8,128)(2,1)}, bf16[4,128,2048]{2,1,0:T(8,128)(2,1)}) custom-call(bf16[4,64,1280]{2,1,0:T(8,128)(2,1)} %maximum_bitcast_fusion.w_ref, bf16[128,2048]{1,0:T(8,128)(2,1)} %wo_ref.1, bf16[128,2048]{1,0:T(8,128)(2,1)} %t_ref.1), custom_call_target="tpu_custom_call" | custom-call | tf_op jit(solution)/shard_map/gather_weights/pallas_call | solution.py:789
  201.2 1.0 fusion.16
  202.2 1.0 pad_maximum_fusion
  204.3 1.2 fusion.11.mask_ref
  205.5 7.0 convolution_multiply_fusion.q_ref.k_ref.v_ref
  212.5 1.4 convert_bitcast_fusion
  214.3 1.3 copy-done.8
  217.0 18.2 %attend.1.o_ref = bf16[512,1024]{1,0:T(8,128)(2,1)} custom-call(f32[512,1280]{1,0:T(8,128)} %convolution_multiply_fusion.q_ref.k_ref.v_ref, f32[512,1280]{1,0:T(8,128)} %convolution_multiply_fusion.q_ref.k_ref.v_ref, f32[512,1280]{1,0:T(8,128)} %convolution_multiply_fusion.q_ref.k_ref.v_ref, f32[1,128]{1,0:T(1,128)} %broadcast_in_dim_reshape.8.gq_ref, ...), custom_call_target="tpu_custom_call" | custom-call | tf_op jit(solution)/shard_map/attend/pallas_call | solution.py:1138
  235.2 3.6 convolution_convert_fusion.2
  238.8 14.4 %pack_reduce.1 = f32[128,2048]{1,0:T(8,128)S(1)} custom-call(bf16[4,128,2048]{2,1,0:T(8,128)(2,1)S(1)} %bitcast.86), custom_call_target="tpu_custom_call" | custom-call | tf_op jit(solution)/shard_map/pack_reduce/pallas_call | solution.py:906
  253.2 1.1 fusion.15
  255.0 0.8 multiply_reduce_fusion.3
  255.8 1.1 fusion.13.sel_ref
  256.9 2.4 fusion.1.selt_ref
  259.3 0.9 multiply_convert_fusion.b_ref
  260.3 1.3 broadcast_in_dim.99.gate_ref
  261.6 244.1 %expert_reduce.1 = (bf16[32,128,2048]{2,1,0:T(8,128)(2,1)}, bf16[2048,2048]{1,0:T(8,128)(2,1)}, bf16[2048,2048]{1,0:T(8,128)(2,1)}, bf16[2048,768]{1,0:T(8,128)(...) custom-call(bf16[128,2048]{1,0:T(8,128)(2,1)} %multiply_convert_fusion.b_ref, ...), custom_call_target="tpu_custom_call" | custom-call | tf_op jit(solution)/shard_map/expert_reduce/pallas_call | solution.py:654
  505.8 2.0 multiply_reduce_fusion.1
  507.9 2.2 fusion.19.t_ref
  510.1 14.8 %pack_gather.1 = bf16[4,128,2048]{2,1,0:T(8,128)(2,1)} custom-call(bf16[128,2048]{1,0:T(8,128)(2,1)} %fusion.19.t_ref), custom_call_target="tpu_custom_call" | custom-call | tf_op jit(solution)/shard_map/pack_gather/pallas_call | solution.py:838
  525.6 0.9 copy.26.inv_ref
  526.6 6.2 convolution_convert_fusion.4.do_ref
  532.7 28.9 %attend_back.1 = (bf16[512,1024]{1,0:T(8,128)(2,1)}, bf16[512,128]{1,0:T(8,128)(2,1)}, bf16[512,128]{1,0:T(8,128)(2,1)}, f32[8,128]{1,0:T(8,128)}, f32[8,128]{1,0:T(8,128)}) custom-call(f32[512,1280]{1,0:T(8,128)} %convolution_multiply_fusion.q_ref.k_ref.v_ref, f32[512,1280]{1,0:T(8,128)} %convolution_multiply_fusion.q_ref.k_ref.v_ref, ...), custom_call_target="tpu_custom_call" | custom-call | tf_op jit(solution)/shard_map/attend_back/pallas_call | solution.py:1153
  561.7 1.5 constant_dynamic-update-slice_fusion.7
  563.3 7.4 convolution_convert_fusion.3
  570.7 9.3 %convolution_bitcast_fusion.1 = f32[1,768,2048]{2,1,0:T(8,128)} fusion(bf16[2048,768]{1,0:T(8,128)(2,1)S(1)} %copy-done.28, bf16[2048,2048]{1,0:T(8,128)(2,1)S(1)} %bitcast.115), kind=kOutput, calls=%fused_computation.3 | convolution fusion | flops 6442450944 | bytes 17825792 | tf_op jit(solution)/shard_map/rf,rd->fd/dot_general | solution.py:1256
  580.1 16.3 %convolution_bitcast_fusion = f32[1,2048,1536]{2,1,0:T(8,128)} fusion(bf16[2048,2048]{1,0:T(8,128)(2,1)S(1)} %bitcast.113, bf16[2048,1536]{1,0:T(8,128)(2,1)S(1)} %bitcast.117), kind=kOutput, calls=%fused_computation | convolution fusion | flops 12884901888 | bytes 27262976 | tf_op jit(solution)/shard_map/rd,rc->dc/dot_general | solution.py:1255
  596.4 0.7 slice_reduce_fusion.1
  597.2 0.7 slice_reduce_fusion
  598.1 0.7 maximum_maximum_fusion.s_ref
  598.9 6.2 convolution_convert_fusion.1
  605.0 4.7 convolution_convert_fusion
  609.7 197.1 %reduce_grads.1 = (f32[128,2048]{1,0:T(8,128)}, f32[4,64,1280]{2,1,0:T(8,128)}, f32[4,8,128]{2,1,0:T(8,128)}, f32[128,2048]{1,0:T(8,128)}) custom-call(bf16[8,128,2048]{2,1,0:T(8,128)(2,1)} %bitcast.92, bf16[32,64,1280]{2,1,0:T(8,128)(2,1)} %bitcast.90, f32[32,8,128]{2,1,0:T(8,128)} %maximum_maximum_fusion.s_ref, bf16[4,128,2048]{2,1,0:T(8,128)(2,1)} %bitcast.102), custom_call_target="tpu_custom_call" | custom-call | tf_op jit(solution)/shard_map/reduce_grads/pallas_call | solution.py:1022
  806.8 1.4 slice_bitcast_fusion
  808.2 1.1 copy.33
  809.4 1.6 fusion.6
  812.0 1.0 slice_bitcast_fusion.1
  813.2 1.9 broadcast_multiply_fusion
  815.1 2.8 fusion.8
  817.9 1.0 copy.54
  (123 shorter events, 9.1 us)
Async XLA Ops:
  7.2 205.3 %all-gather.6.cloned.1.call-start = ((), (), s32[]{:S(2)}) async-start(), calls=%async_computation.3 | async-start | bytes 1081344 | tf_op jit(solution)/shard_map/all_gather | solution.py:1211
  13.2 247.1 %all-gather.4.cloned.1.call-start = ((), (), s32[]{:S(2)}) async-start(), calls=%async_computation.1 | async-start | bytes 17301504 | tf_op jit(solution)/shard_map/all_gather | solution.py:1212
  13.9 801.1 %reduce-scatter.2.cloned.1.call-start = ((), (), s32[]{:S(2)}) async-start(), calls=%async_computation.2 | async-start | bytes 17301504 | tf_op jit(solution)/shard_map/reduce_scatter | solution.py:1264
  14.6 1.3 copy-start.24
  16.0 184.9 %copy-start.19 = (s32[1,512]{1,0:T(1,128)S(1)}, s32[1,512]{1,0:T(1,128)}, u32[]{:S(2)}) copy-start(s32[1,512]{1,0:T(1,128)} %param.15) | copy-start | bytes 6148
  200.9 2.3 copy-start.10
  214.3 1.3 copy-start.8
  217.0 18.3 %copy-start.27 = (bf16[8,128,2048]{2,1,0:T(8,128)(2,1)S(1)}, bf16[8,128,2048]{2,1,0:T(8,128)(2,1)}, u32[]{:S(2)}) copy-start(bf16[8,128,2048]{2,1,0:T(8,128)(2,1)} %get-tuple-element.35) | copy-start | bytes 12582916
  238.8 16.2 %copy-start.3 = (bf16[128,2048]{1,0:T(8,128)(2,1)S(1)}, bf16[128,2048]{1,0:T(8,128)(2,1)}, u32[]{:S(2)}) copy-start(bf16[128,2048]{1,0:T(8,128)(2,1)} %t_ref.1) | copy-start | bytes 1572868
  253.2 6.1 copy-start.15
  255.8 3.6 copy-start
  255.8 5.8 copy-start.22
  505.7 2.1 copy-start.1
  505.7 2.2 copy-start.2
  505.7 2.2 copy-start.16
  505.8 2.2 copy-start.23
  524.9 0.7 copy-start.21
  525.0 1.6 copy-start.26
  561.6 1.5 copy-start.18
  561.6 1.5 copy-start.17
  561.6 9.1 %slice-start.2 = ((s8[8388608]{0:T(1024)(128)(4,1)}), s8[4194304]{0:T(1024)(128)(4,1)S(1)}, s32[]{:S(2)}) async-start(s8[8388608]{0:T(1024)(128)(4,1)} %bitcast.114), calls=%async_computation.6 | async-start | bytes 8388608
  563.2 7.5 copy-start.13
  563.2 7.5 slice-start.3
  563.2 7.5 copy-start.28
  563.3 16.8 %slice-start = ((s8[8388608]{0:T(1024)(128)(4,1)}), s8[4194304]{0:T(1024)(128)(4,1)S(1)}, s32[]{:S(2)}) async-start(s8[8388608]{0:T(1024)(128)(4,1)} %bitcast.112), calls=%async_computation.4 | async-start | bytes 8388608
  563.3 16.8 %slice-start.4 = ((s8[6291456]{0:T(1024)(128)(4,1)}), s8[4194304]{0:T(1024)(128)(4,1)S(1)}, s32[]{:S(2)}) async-start(s8[6291456]{0:T(1024)(128)(4,1)} %bitcast.116), calls=%async_computation.8 | async-start | bytes 8388608
  570.7 9.3 %slice-start.1 = ((s8[8388608]{0:T(1024)(128)(4,1)}), s8[4194304]{0:T(1024)(128)(4,1)S(1)}, s32[]{:S(2)}) async-start(s8[8388608]{0:T(1024)(128)(4,1)} %bitcast.112), calls=%async_computation.5 | async-start | bytes 8388608
  570.7 9.3 %slice-start.5 = ((s8[6291456]{0:T(1024)(128)(4,1)}), s8[2097152]{0:T(1024)(128)(4,1)S(1)}, s32[]{:S(2)}) async-start(s8[6291456]{0:T(1024)(128)(4,1)} %bitcast.116), calls=%async_computation.9 | async-start | bytes 4194304
  580.1 18.8 %copy-start.7 = (bf16[512,1024]{1,0:T(8,128)(2,1)S(1)}, bf16[512,1024]{1,0:T(8,128)(2,1)}, u32[]{:S(2)}) copy-start(bf16[512,1024]{1,0:T(8,128)(2,1)} %attend.1.o_ref) | copy-start | bytes 3145732
  598.9 6.2 copy-start.11
  598.9 6.2 copy-start.14
  806.8 2.5 copy-start.20
  806.8 2.5 copy-start.4
  809.3 3.7 copy-start.6
  809.4 3.8 copy-start.9
  809.4 3.8 copy-start.25
  813.1 1.9 copy-start.5
  815.1 2.8 copy-start.12
Sparse Core Ops, SparseCore 0:
  13.3 102.0 all-gather.5
  118.3 141.8 all-gather.3
  525.1 228.8 reduce-scatter.1

commit v3 on v2

--- a/solution.py
+++ b/solution.py
@@ -1260,7 +1260,6 @@
     residual = out_grad.astype(f32) + hidden_inverse * (
         scaled_grad - hidden_norm * jnp.mean(scaled_grad * hidden_norm, axis=-1, keepdims=True))
     residual_pack = pack_gather(residual.astype(bf), 6).reshape(length, width)
-    out_terms, residual_pack = lax.optimization_barrier((out_terms, residual_pack))
     moe_sum = lax.psum_scatter(out_terms.reshape(nd * rows, width), both, scatter_dimension=0, tiled=True).astype(f32)
     block_output = (hidden_state + moe_sum).astype(bf)
     out_term = jnp.einsum("tc,td->cd", attn_flat, residual_pack, preferred_element_type=f32).astype(bf)

time: 831 us -> 833 us (level)
    pallas_call x1, Pallas kernels: 14.8 us -> 32.7 us  [pack_gather(): pl.pallas_call(pack_gather_kernel, out_shape=jax.ShapeDtypeStruct((ny * 2...]
    pallas_call x1, Pallas kernels: 197 us -> 183 us  [reduce_grads(): pl.pallas_call(grads_kernel, out_shape=(jax.ShapeDtypeStruct((rows_o, wid...]
  transfers between devices with their start and end apart: 3 -> 3, of which waited for: 0 -> 0; matrix products, arithmetic and copies ran while one was open for 11% -> 11% of each run, Pallas kernels for 54% -> 56%
where the time goes in v3:
time: 833 us; the launch traced here: 827 us
  Pallas kernels  705 us (85%)
  matrix products  61.2 us (7%)
  other arithmetic  27.1 us (3%)
  local copies, waits for them, and re-layouts  17.9 us (2%)
  between operations  14.5 us (2%)
    pallas_call x1, Pallas kernels, expert_reduce(): pl.pallas_call(expert_reduce_kernel, out_shape=(sds((nd, rows, width), bf...  244 us
    pallas_call x1, Pallas kernels, gather_weights(): pl.pallas_call(weights_kernel, out_shape=(jax.ShapeDtypeStruct((ne * ns,)...  184 us
    pallas_call x1, Pallas kernels, reduce_grads(): pl.pallas_call(grads_kernel, out_shape=(jax.ShapeDtypeStruct((rows_o, wid...  183 us
    pallas_call x1, Pallas kernels, pack_gather(): pl.pallas_call(pack_gather_kernel, out_shape=jax.ShapeDtypeStruct((ny * 2...  32.7 us
    pallas_call x1, Pallas kernels, attend_back(): pl.pallas_call(functools.partial(attend_back_kernel, per), grid=(heads,),...  28.9 us
    pallas_call x1, Pallas kernels, attend(): pl.pallas_call(attend_kernel, grid=(heads,), out_shape=jax.ShapeDtypeStru...  18.3 us
  transfers between devices with their start and end apart: 3, of which 0 were waited for; matrix products, arithmetic and copies ran while one was open for 11% of the time, Pallas kernels for 56%

profile of v3, /device:TPU:2, one launch (start us, length us, event | category | flops | bytes accessed | tf_op | source)
XLA Modules:
  0.0 826.8 jit_solution(4517008567854343961)
XLA Ops:
  7.2 0.7 constant_dynamic-update-slice_fusion.4
  7.9 0.7 constant_dynamic-update-slice_fusion.3
  8.6 0.8 constant_dynamic-update-slice_fusion.2
  9.4 0.8 constant_dynamic-update-slice_fusion.1
  10.8 0.8 dynamic_update_slice.12
  11.7 0.9 dynamic_update_slice.13
  13.2 0.7 all-gather.4.cloned.1.call-update
  14.6 1.3 fusion.2
  16.1 0.9 maximum_bitcast_fusion.w_ref
  17.0 183.9 %gather_weights.1 = (bf16[32,64,1280]{2,1,0:T(8,128)(2,1)}, bf16[8,128,2048]{2,1,0:T(8,128)(2,1)}, bf16[4,128,2048]{2,1,0:T(8,128)(2,1)}) custom-call(bf16[4,64,1280]{2,1,0:T(8,128)(2,1)} %maximum_bitcast_fusion.w_ref, bf16[128,2048]{1,0:T(8,128)(2,1)} %wo_ref.1, bf16[128,2048]{1,0:T(8,128)(2,1)} %t_ref.1), custom_call_target="tpu_custom_call" | custom-call | tf_op jit(solution)/shard_map/gather_weights/pallas_call | solution.py:789
  201.2 1.0 fusion.16
  202.2 1.0 pad_maximum_fusion
  204.3 1.2 fusion.11.mask_ref
  205.5 7.0 convolution_multiply_fusion.q_ref.k_ref.v_ref
  212.5 1.4 convert_bitcast_fusion
  214.3 1.3 copy-done.7
  216.9 18.3 %attend.1.o_ref = bf16[512,1024]{1,0:T(8,128)(2,1)} custom-call(f32[512,1280]{1,0:T(8,128)} %convolution_multiply_fusion.q_ref.k_ref.v_ref, f32[512,1280]{1,0:T(8,128)} %convolution_multiply_fusion.q_ref.k_ref.v_ref, f32[512,1280]{1,0:T(8,128)} %convolution_multiply_fusion.q_ref.k_ref.v_ref, f32[1,128]{1,0:T(1,128)} %broadcast_in_dim_reshape.8.gq_ref, ...), custom_call_target="tpu_custom_call" | custom-call | tf_op jit(solution)/shard_map/attend/pallas_call | solution.py:1138
  235.2 3.6 convolution_convert_fusion.2
  238.8 14.4 %pack_reduce.1 = f32[128,2048]{1,0:T(8,128)S(1)} custom-call(bf16[4,128,2048]{2,1,0:T(8,128)(2,1)S(1)} %bitcast.86), custom_call_target="tpu_custom_call" | custom-call | tf_op jit(solution)/shard_map/pack_reduce/pallas_call | solution.py:906
  253.2 1.1 fusion.15
  254.9 0.8 multiply_reduce_fusion.3
  255.7 1.1 fusion.13.sel_ref
  256.9 2.4 fusion.1.selt_ref
  259.3 0.9 multiply_convert_fusion.b_ref
  260.3 1.3 broadcast_in_dim.99.gate_ref
  261.6 244.1 %expert_reduce.1 = (bf16[32,128,2048]{2,1,0:T(8,128)(2,1)}, bf16[2048,2048]{1,0:T(8,128)(2,1)}, bf16[2048,2048]{1,0:T(8,128)(2,1)}, bf16[2048,768]{1,0:T(8,128)(...) custom-call(bf16[128,2048]{1,0:T(8,128)(2,1)} %multiply_convert_fusion.b_ref, ...), custom_call_target="tpu_custom_call" | custom-call | tf_op jit(solution)/shard_map/expert_reduce/pallas_call | solution.py:654
  506.3 0.9 copy.26.inv_ref
  507.7 1.1 fusion.19.t_ref
  508.8 32.7 %pack_gather.1 = bf16[4,128,2048]{2,1,0:T(8,128)(2,1)} custom-call(bf16[128,2048]{1,0:T(8,128)(2,1)} %fusion.19.t_ref), custom_call_target="tpu_custom_call" | custom-call | tf_op jit(solution)/shard_map/pack_gather/pallas_call | solution.py:838
  541.5 6.2 convolution_convert_fusion.4.do_ref
  547.8 28.9 %attend_back.1 = (bf16[512,1024]{1,0:T(8,128)(2,1)}, bf16[512,128]{1,0:T(8,128)(2,1)}, bf16[512,128]{1,0:T(8,128)(2,1)}, f32[8,128]{1,0:T(8,128)}, f32[8,128]{1,0:T(8,128)}) custom-call(f32[512,1280]{1,0:T(8,128)} %convolution_multiply_fusion.q_ref.k_ref.v_ref, f32[512,1280]{1,0:T(8,128)} %convolution_multiply_fusion.q_ref.k_ref.v_ref, ...), custom_call_target="tpu_custom_call" | custom-call | tf_op jit(solution)/shard_map/attend_back/pallas_call | solution.py:1153
  576.7 1.5 constant_dynamic-update-slice_fusion.7
  578.3 7.4 convolution_convert_fusion.3
  585.8 9.3 %convolution_bitcast_fusion.1 = f32[1,768,2048]{2,1,0:T(8,128)} fusion(bf16[2048,768]{1,0:T(8,128)(2,1)S(1)} %copy-done.27, bf16[2048,2048]{1,0:T(8,128)(2,1)S(1)} %bitcast.115), kind=kOutput, calls=%fused_computation.3 | convolution fusion | flops 6442450944 | bytes 17825792 | tf_op jit(solution)/shard_map/rf,rd->fd/dot_general | solution.py:1256
  595.1 16.3 %convolution_bitcast_fusion = f32[1,2048,1536]{2,1,0:T(8,128)} fusion(bf16[2048,2048]{1,0:T(8,128)(2,1)S(1)} %bitcast.113, bf16[2048,1536]{1,0:T(8,128)(2,1)S(1)} %bitcast.117), kind=kOutput, calls=%fused_computation | convolution fusion | flops 12884901888 | bytes 27262976 | tf_op jit(solution)/shard_map/rd,rc->dc/dot_general | solution.py:1255
  611.5 0.7 slice_reduce_fusion.1
  612.3 0.7 slice_reduce_fusion
  613.2 0.7 maximum_maximum_fusion.s_ref
  613.9 6.5 convolution_convert_fusion.1
  620.4 4.7 convolution_convert_fusion
  625.1 183.0 %reduce_grads.1 = (f32[128,2048]{1,0:T(8,128)}, f32[4,64,1280]{2,1,0:T(8,128)}, f32[4,8,128]{2,1,0:T(8,128)}, f32[128,2048]{1,0:T(8,128)}) custom-call(bf16[8,128,2048]{2,1,0:T(8,128)(2,1)} %bitcast.92, bf16[32,64,1280]{2,1,0:T(8,128)(2,1)} %bitcast.90, f32[32,8,128]{2,1,0:T(8,128)} %maximum_maximum_fusion.s_ref, bf16[4,128,2048]{2,1,0:T(8,128)(2,1)} %bitcast.102), custom_call_target="tpu_custom_call" | custom-call | tf_op jit(solution)/shard_map/reduce_grads/pallas_call | solution.py:1022
  808.1 1.4 slice_bitcast_fusion
  809.5 1.1 copy.33
  810.7 1.6 fusion.6
  813.3 1.0 slice_bitcast_fusion.1
  814.5 1.9 broadcast_multiply_fusion
  816.4 2.8 fusion.8
  819.2 1.0 copy.54
  (121 shorter events, 8.6 us)
Async XLA Ops:
  7.2 205.3 %all-gather.6.cloned.1.call-start = ((), (), s32[]{:S(2)}) async-start(), calls=%async_computation.3 | async-start | bytes 1081344 | tf_op jit(solution)/shard_map/all_gather | solution.py:1211
  13.2 247.1 %all-gather.4.cloned.1.call-start = ((), (), s32[]{:S(2)}) async-start(), calls=%async_computation.1 | async-start | bytes 17301504 | tf_op jit(solution)/shard_map/all_gather | solution.py:1212
  13.9 802.4 %reduce-scatter.2.cloned.1.call-start = ((), (), s32[]{:S(2)}) async-start(), calls=%async_computation.2 | async-start | bytes 17301504 | tf_op jit(solution)/shard_map/reduce_scatter | solution.py:1263
  14.6 1.3 copy-start.23
  16.0 184.9 %copy-start.18 = (s32[1,512]{1,0:T(1,128)S(1)}, s32[1,512]{1,0:T(1,128)}, u32[]{:S(2)}) copy-start(s32[1,512]{1,0:T(1,128)} %param.15) | copy-start | bytes 6148
  200.9 2.3 copy-start.9
  214.3 1.3 copy-start.7
  216.9 18.3 %copy-start.26 = (bf16[8,128,2048]{2,1,0:T(8,128)(2,1)S(1)}, bf16[8,128,2048]{2,1,0:T(8,128)(2,1)}, u32[]{:S(2)}) copy-start(bf16[8,128,2048]{2,1,0:T(8,128)(2,1)} %get-tuple-element.33) | copy-start | bytes 12582916
  238.8 16.2 %copy-start.3 = (bf16[128,2048]{1,0:T(8,128)(2,1)S(1)}, bf16[128,2048]{1,0:T(8,128)(2,1)}, u32[]{:S(2)}) copy-start(bf16[128,2048]{1,0:T(8,128)(2,1)} %t_ref.1) | copy-start | bytes 1572868
  253.2 6.1 copy-start.14
  255.7 3.6 copy-start
  255.7 5.8 copy-start.21
  505.7 0.7 copy-start.20
  505.7 1.6 copy-start.25
  505.7 1.6 copy-start.1
  505.7 1.6 copy-start.2
  505.7 1.6 copy-start.15
  505.7 1.6 copy-start.22
  505.8 1.9 copy-start.5
  576.7 1.5 copy-start.17
  576.7 1.5 copy-start.16
  576.7 9.1 %slice-start.2 = ((s8[8388608]{0:T(1024)(128)(4,1)}), s8[4194304]{0:T(1024)(128)(4,1)S(1)}, s32[]{:S(2)}) async-start(s8[8388608]{0:T(1024)(128)(4,1)} %bitcast.114), calls=%async_computation.6 | async-start | bytes 8388608
  578.3 7.5 copy-start.12
  578.3 7.5 slice-start.3
  578.3 7.5 copy-start.27
  578.3 16.8 %slice-start = ((s8[8388608]{0:T(1024)(128)(4,1)}), s8[4194304]{0:T(1024)(128)(4,1)S(1)}, s32[]{:S(2)}) async-start(s8[8388608]{0:T(1024)(128)(4,1)} %bitcast.112), calls=%async_computation.4 | async-start | bytes 8388608
  578.3 16.8 %slice-start.4 = ((s8[6291456]{0:T(1024)(128)(4,1)}), s8[4194304]{0:T(1024)(128)(4,1)S(1)}, s32[]{:S(2)}) async-start(s8[6291456]{0:T(1024)(128)(4,1)} %bitcast.116), calls=%async_computation.8 | async-start | bytes 8388608
  585.8 9.3 %slice-start.1 = ((s8[8388608]{0:T(1024)(128)(4,1)}), s8[4194304]{0:T(1024)(128)(4,1)S(1)}, s32[]{:S(2)}) async-start(s8[8388608]{0:T(1024)(128)(4,1)} %bitcast.112), calls=%async_computation.5 | async-start | bytes 8388608
  585.8 9.3 %slice-start.5 = ((s8[6291456]{0:T(1024)(128)(4,1)}), s8[2097152]{0:T(1024)(128)(4,1)S(1)}, s32[]{:S(2)}) async-start(s8[6291456]{0:T(1024)(128)(4,1)} %bitcast.116), calls=%async_computation.9 | async-start | bytes 4194304
  613.9 6.5 copy-start.10
  613.9 6.5 copy-start.13
  808.1 2.5 copy-start.19
  808.1 2.5 copy-start.4
  810.6 3.7 copy-start.6
  810.6 3.8 copy-start.8
  810.7 3.8 copy-start.24
  816.4 2.8 copy-start.11
Sparse Core Ops, SparseCore 0:
  13.3 102.0 all-gather.5
  118.3 141.8 all-gather.3
  505.9 225.1 reduce-scatter.1
